TPU v7x, 32 devices: a whole 2x2x4 slice. The times are simulated.
32 devices in a mesh: member: 8 (over y, x, core), lat: 4 (over z).
Axes of the slice: x: 2, y: 2, z: 4, core: 2. Of those that a mesh axis runs over, the one named last changes fastest.
Arguments:
- starting_state_array: bfloat16 [8, 640, 4, 2560], P('member', 'lat'), may hold values from -6 to 6
- stochastic_forcing_array: bfloat16 [8, 640, 4, 2560], P('member', 'lat'), may hold values from -2 to 2
- decoded_outlook_array: bfloat16 [8, 640, 4, 2560], P('member', 'lat'), may hold values from -6 to 6
- truth_analysis_array: bfloat16 [640, 4, 2560], P('lat'), may hold values from -6 to 6
- weighted_polynomial_basis: bfloat16 [320, 640, 320], P('lat'), may hold values from -0.25 to 0.25
- wavenumber_attenuation: float32 [320], replicated, may hold values from 0.05 to 0.5
Outputs:
- advanced: bfloat16 [8, 640, 4, 2560], P('member', 'lat')
- adjoint: bfloat16 [8, 640, 4, 2560], P('member', 'lat')
All inputs are finite; a program needn't handle non-finite values.
Results may differ from a plain program's by a relative error of at most 0.0081.
Values may be sent and summed in bfloat16 or wider, within the bound.
No kernel may reach another device: no remote copies, remote signals or barrier semaphores. Data moves between devices by JAX's collectives and lax.ppermute only.
A program may use at most 192 MiB of HBM per device.

v0:
```python
import math

import jax
import jax.numpy as jnp
from jax import lax
from jax.sharding import PartitionSpec as P

EASTWARD_TALLY = 2560
KM = 320


def fourier_table(lon, waves):
    cols = lax.broadcasted_iota(jnp.int32, (lon, 2 * waves), 1)
    rows = lax.broadcasted_iota(jnp.int32, (lon, 2 * waves), 0)
    wave = cols // 2
    phase = (wave * rows % lon).astype(jnp.float32) * (2.0 * math.pi / lon)
    value = jnp.where(cols % 2 == 0, jnp.cos(phase), jnp.sin(phase))
    return (value * math.sqrt(2.0 / lon)).astype(jnp.bfloat16)


def spectral_filter(field, table, weighted_polynomial_basis, wavenumber_attenuation):
    count, rows, level_count, lon = field.shape
    width = table.shape[1]
    coeffs = jnp.dot(
        field.reshape(count * rows * level_count, lon), table, preferred_element_type=jnp.float32
    )
    coeffs = coeffs.astype(jnp.bfloat16).reshape(count, rows, level_count, width)
    by_lat = lax.all_to_all(coeffs, "lat", split_axis=3, concat_axis=1, tiled=True)
    waves = weighted_polynomial_basis.shape[0]
    by_lat = by_lat.reshape(count, by_lat.shape[1], level_count, waves, 2)
    spectra = jnp.einsum(
        "mln,blemp->bmnep", weighted_polynomial_basis, by_lat, preferred_element_type=jnp.float32
    )
    spectra = (spectra * wavenumber_attenuation[None, None, :, None, None]).astype(jnp.bfloat16)
    synthesis = jnp.einsum(
        "mln,bmnep->blemp", weighted_polynomial_basis, spectra, preferred_element_type=jnp.float32
    )
    synthesis = synthesis.astype(jnp.bfloat16).reshape(
        count, by_lat.shape[1], level_count, waves * 2
    )
    returned = lax.all_to_all(synthesis, "lat", split_axis=1, concat_axis=3, tiled=True)
    grid = jnp.dot(
        returned.reshape(count * rows * level_count, width),
        table.T,
        preferred_element_type=jnp.float32,
    )
    return grid.reshape(count, rows, level_count, lon)


def per_device(
    starting_state_array,
    stochastic_forcing_array,
    decoded_outlook_array,
    truth_analysis_array,
    weighted_polynomial_basis,
    wavenumber_attenuation,
):
    table = fourier_table(EASTWARD_TALLY, KM)
    members = lax.axis_size("member")
    local_realisation = decoded_outlook_array[0].astype(jnp.float32)
    stepped = spectral_filter(
        starting_state_array, table, weighted_polynomial_basis, wavenumber_attenuation
    )
    sorted_positions = jnp.sum(
        jnp.sign(
            local_realisation[None]
            - lax.all_gather(decoded_outlook_array, "member", axis=0, tiled=True).astype(
                jnp.float32
            )
        ),
        axis=0,
    )
    score_derivative = (
        jnp.sign(local_realisation - truth_analysis_array.astype(jnp.float32))
        - sorted_positions / (members - 1)
    ).astype(jnp.bfloat16)
    carried = spectral_filter(
        score_derivative[None], table, weighted_polynomial_basis, wavenumber_attenuation
    )
    advanced = (stepped + stochastic_forcing_array.astype(jnp.float32)).astype(jnp.bfloat16)
    return (advanced, carried.astype(jnp.bfloat16))


def solution(mesh):
    return jax.shard_map(
        per_device,
        mesh=mesh,
        in_specs=(
            P("member", "lat", None, None),
            P("member", "lat", None, None),
            P("member", "lat", None, None),
            P("lat", None, None),
            P("lat", None, None),
            P(),
        ),
        out_specs=(P("member", "lat", None, None), P("member", "lat", None, None)),
        check_vma=False,
    )
```

profile of v0, /device:TPU:0, one launch (start us, length us, event | category | flops | bytes accessed | tf_op | source)
XLA Modules:
  0.0 375.3 jit_solution(16038108212285226642)
XLA Ops:
  7.2 0.0 copy-start.1
  7.2 0.0 all-gather.2.cloned.1.call-start
  7.2 7.1 %bitcast_convert_fusion = (f32[160,4,2560]{2,0,1:T(8,128)}, bf16[1,160,4,2560]{3,1,2,0:T(8,128)(2,1)}) fusion(bf16[1,160,4,2560]{3,2,1,0:T(4,128)(2,1)} %param.8), kind=kLoop, calls=%fused_computation.23 | loop fusion | flops 1638400 | bytes 13107200 | tf_op jit(solution)/shard_map/convert_element_type | solution.py:60
  14.3 0.0 all-gather.2.cloned.1.call-update
  14.3 0.0 copy-done.1
  14.3 3.0 reshape.65
  17.3 33.2 %fusion.29 = bf16[640,640]{1,0:T(8,128)(2,1)S(1)} fusion(bf16[640,2560]{1,0:T(8,128)(2,1)} %reshape.65, s32[640]{0:T(1024)S(1)} %get-tuple-element.12, s32[640]{0:T(1024)S(1)} %get-tuple-element.15, s32[640]{0:T(1024)S(1)} %get-tuple-element.13, s32[640]{0:T(1024)S(1)} %get-tuple-element.14, pred[640]{0:T(1024)(128)(4,1)S(1)} %get-tuple-element.16, ...), kind=kOutput, calls=%fused_computation.36 | convolution fusion | flops 2122137600 | bytes 4107520 | tf_op jit(solution)/shard_map/dot_general | solution.py:24
  50.5 0.0 copy-start.2
  50.5 0.2 reshape.66
  50.7 2.2 copy.42
  52.9 38.0 %all_to_all.60 = bf16[1,160,4,640]{1,2,0,3:T(4,128)(2,1)S(1)} all-to-all(bf16[1,160,4,640]{1,2,0,3:T(4,128)(2,1)S(1)} %copy.42), channel_id=1, replica_groups=mesh['member'=8,'lat'=4] {'lat'}, dimensions={3} | all-to-all | bytes 1638400 | tf_op jit(solution)/shard_map/all_to_all | solution.py:28
  90.9 1.7 copy.71
  92.6 1.2 reshape.67
  93.8 0.0 copy-done.2
  93.8 29.4 %fusion.17 = bf16[80,4,2,640]{3,1,2,0:T(4,128)(2,1)S(1)} fusion(bf16[80,640,320]{1,2,0:T(8,128)(2,1)} %param.10, bf16[640,4,80,2]{0,1,3,2:T(4,128)(2,1)S(1)} %reshape.67, f32[320]{0:T(512)S(1)} %copy-done.2), kind=kOutput, calls=%fused_computation.26 | convolution fusion | flops 525107200 | bytes 34407680 | tf_op jit(solution)/shard_map/mln,bmnep->blemp/dot_general | solution.py:35
  123.2 2.7 copy.44
  125.9 4.3 %all-to-all-start.1 = ((bf16[1,640,4,160]{3,2,0,1:T(4,128)(2,1)}), bf16[1,640,4,160]{3,2,0,1:T(4,128)(2,1)}, u32[]{:S(2)}, u32[]{:S(2)}) async-start(bf16[1,640,4,160]{3,2,0,1:T(4,128)(2,1)} %copy.44), calls=%async_computation.1 | async-start | bytes 2621440 | tf_op jit(solution)/shard_map/all_to_all | solution.py:41
  130.2 16.7 %all-gather.2.cloned.1.call-done = bf16[8,160,4,2560]{3,1,2,0:T(8,128)(2,1)} async-done(((bf16[1,160,4,2560]{3,1,2,0:T(8,128)(2,1)}), bf16[8,160,4,2560]{3,1,2,0:T(8,128)(2,1)}) %all-gather.2.cloned.1.call-update) | async-done | bytes 26214416 | tf_op jit(solution)/shard_map/all_gather | solution.py:67
  146.9 0.0 copy-start
  146.9 26.1 %sign_reduce_fusion = f32[160,4,2560]{2,0,1:T(8,128)} fusion(bf16[8,160,4,2560]{3,1,2,0:T(8,128)(2,1)} %all-gather.2.cloned.1.call-done, f32[160,4,2560]{2,0,1:T(8,128)} %get-tuple-element.10), kind=kLoop, calls=%fused_computation | loop fusion | flops 50790400 | bytes 39321600 | tf_op jit(solution)/shard_map/reduce_sum | solution.py:64
  173.0 0.0 copy-done
  173.0 5.4 %subtract_convert_fusion = bf16[160,4,2560]{2,0,1:T(8,128)(2,1)S(1)} fusion(f32[160,4,2560]{2,0,1:T(8,128)} %sign_reduce_fusion, bf16[160,4,2560]{2,1,0:T(4,128)(2,1)} %param.9, bf16[1,160,4,2560]{3,2,1,0:T(4,128)(2,1)S(1)} %copy-done), kind=kLoop, calls=%fused_computation.14 | loop fusion | flops 11468800 | bytes 16384000 | tf_op jit(solution)/shard_map/convert_element_type | solution.py:76
  178.3 2.5 copy.50
  180.9 3.0 reshape_broadcast_in_dim.3
  183.8 33.3 %convolution_convert_fusion.2 = bf16[640,640]{1,0:T(8,128)(2,1)S(1)} fusion(bf16[640,2560]{1,0:T(8,128)(2,1)} %reshape_broadcast_in_dim.3, s32[640]{0:T(1024)S(1)} %get-tuple-element.12, s32[640]{0:T(1024)S(1)} %get-tuple-element.15, s32[640]{0:T(1024)S(1)} %get-tuple-element.13, s32[640]{0:T(1024)S(1)} %get-tuple-element.14, ...), kind=kOutput, calls=%fused_computation.29 | convolution fusion | flops 2122137600 | bytes 4107520 | tf_op jit(solution)/shard_map/dot_general | solution.py:24
  217.2 0.2 reshape.71
  217.3 2.6 copy.51
  220.0 0.0 all-to-all-done.1
  220.0 4.6 %all-to-all-start.2 = ((bf16[1,160,4,640]{1,2,0,3:T(4,128)(2,1)}), bf16[1,160,4,640]{1,2,0,3:T(4,128)(2,1)S(1)}, u32[]{:S(2)}, u32[]{:S(2)}) async-start(bf16[1,160,4,640]{1,2,0,3:T(4,128)(2,1)} %copy.51), calls=%async_computation.2 | async-start | bytes 2621440 | tf_op jit(solution)/shard_map/all_to_all | solution.py:28
  224.6 2.3 copy.70
  226.9 0.8 reshape.70
  227.8 28.6 %all-to-all-done.2 = bf16[1,160,4,640]{1,2,0,3:T(4,128)(2,1)S(1)} async-done(((bf16[1,160,4,640]{1,2,0,3:T(4,128)(2,1)}), bf16[1,160,4,640]{1,2,0,3:T(4,128)(2,1)S(1)}, u32[]{:S(2)}, u32[]{:S(2)}) %all-to-all-start.2) | async-done | bytes 819232 | tf_op jit(solution)/shard_map/all_to_all | solution.py:28
  256.3 1.7 copy.69
  258.0 1.2 reshape.72
  259.2 29.4 %fusion.20 = bf16[80,4,2,640]{3,1,2,0:T(4,128)(2,1)S(1)} fusion(bf16[80,640,320]{1,2,0:T(8,128)(2,1)} %param.10, bf16[640,4,80,2]{0,1,3,2:T(4,128)(2,1)S(1)} %reshape.72, f32[320]{0:T(512)S(1)} %copy-done.2), kind=kOutput, calls=%fused_computation.27 | convolution fusion | flops 525107200 | bytes 34407680 | tf_op jit(solution)/shard_map/mln,bmnep->blemp/dot_general | solution.py:35
  288.6 2.6 copy.53
  291.3 3.8 all-to-all-start.3
  295.0 31.8 %fusion.10 = bf16[1,160,4,2560]{3,1,2,0:T(8,128)(2,1)S(1)} fusion(bf16[160,4,640]{2,0,1:T(8,128)(2,1)S(1)} %reshape.70, bf16[1,160,4,2560]{3,2,1,0:T(4,128)(2,1)} %param.7, s32[640]{0:T(1024)S(1)} %get-tuple-element.12, s32[640]{0:T(1024)S(1)} %get-tuple-element.15, s32[640]{0:T(1024)S(1)} %get-tuple-element.13, s32[640]{0:T(1024)S(1)} %get-tuple-element.14, ...), kind=kOutput, calls=%fused_computation.13 | convolution fusion | flops 2126643200 | bytes 7384320 | tf_op jit(solution)/shard_map/dot_general | solution.py:42
  326.9 4.2 %copy.55 = bf16[1,160,4,2560]{3,2,1,0:T(4,128)(2,1)} copy(bf16[1,160,4,2560]{3,1,2,0:T(8,128)(2,1)S(1)} %fusion.10) | data formatting | bytes 6553600
  331.1 0.0 all-to-all-done.3
  331.1 1.0 copy.68
  332.1 0.8 dot_general.42
  333.0 31.0 %fusion.14 = bf16[1,160,4,2560]{3,1,2,0:T(8,128)(2,1)S(1)} fusion(bf16[160,4,640]{2,0,1:T(8,128)(2,1)S(1)} %dot_general.42, s32[640]{0:T(1024)S(1)} %get-tuple-element.12, s32[640]{0:T(1024)S(1)} %get-tuple-element.15, s32[640]{0:T(1024)S(1)} %get-tuple-element.13, s32[640]{0:T(1024)S(1)} %get-tuple-element.14, pred[640]{0:T(1024)(128)(4,1)S(1)} %get-tuple-element.16, ...), kind=kOutput, calls=%fused_computation.22 | convolution fusion | flops 2123366400 | bytes 4107520 | tf_op jit(solution)/shard_map/dot_general | solution.py:42
  364.0 4.2 %copy.56 = bf16[1,160,4,2560]{3,2,1,0:T(4,128)(2,1)} copy(bf16[1,160,4,2560]{3,1,2,0:T(8,128)(2,1)S(1)} %fusion.14) | data formatting | bytes 6553600
  (3 shorter events, 0.0 us)
Async XLA Ops:
  7.2 7.1 %copy-start.1 = (bf16[1,160,4,2560]{3,2,1,0:T(4,128)(2,1)S(1)}, bf16[1,160,4,2560]{3,2,1,0:T(4,128)(2,1)}, u32[]{:S(2)}) copy-start(bf16[1,160,4,2560]{3,2,1,0:T(4,128)(2,1)} %param.6) | copy-start | bytes 9830404
  7.2 139.7 %all-gather.2.cloned.1.call-start = ((), (), s32[]{:S(2)}) async-start(), calls=%async_computation.4 | async-start | bytes 29491200 | tf_op jit(solution)/shard_map/all_gather | solution.py:67
  50.5 43.3 %copy-start.2 = (f32[320]{0:T(512)S(1)}, f32[320]{0:T(512)}, u32[]{:S(2)}) copy-start(f32[320]{0:T(512)} %param.11) | copy-start | bytes 3844
  125.9 94.1 %all-to-all-start.1 = ((bf16[1,640,4,160]{3,2,0,1:T(4,128)(2,1)}), bf16[1,640,4,160]{3,2,0,1:T(4,128)(2,1)}, u32[]{:S(2)}, u32[]{:S(2)}) async-start(bf16[1,640,4,160]{3,2,0,1:T(4,128)(2,1)} %copy.44), calls=%async_computation.1 | async-start | bytes 2621440 | tf_op jit(solution)/shard_map/all_to_all | solution.py:41
  146.9 26.1 %copy-start = (bf16[1,160,4,2560]{3,2,1,0:T(4,128)(2,1)S(1)}, bf16[1,160,4,2560]{3,2,1,0:T(4,128)(2,1)}, u32[]{:S(2)}) copy-start(bf16[1,160,4,2560]{3,2,1,0:T(4,128)(2,1)} %param.8) | copy-start | bytes 9830404
  220.0 36.4 %all-to-all-start.2 = ((bf16[1,160,4,640]{1,2,0,3:T(4,128)(2,1)}), bf16[1,160,4,640]{1,2,0,3:T(4,128)(2,1)S(1)}, u32[]{:S(2)}, u32[]{:S(2)}) async-start(bf16[1,160,4,640]{1,2,0,3:T(4,128)(2,1)} %copy.51), calls=%async_computation.2 | async-start | bytes 2621440 | tf_op jit(solution)/shard_map/all_to_all | solution.py:28
  291.3 39.9 %all-to-all-start.3 = ((bf16[1,640,4,160]{3,2,0,1:T(4,128)(2,1)}), bf16[1,640,4,160]{3,2,0,1:T(4,128)(2,1)S(1)}, u32[]{:S(2)}, u32[]{:S(2)}) async-start(bf16[1,640,4,160]{3,2,0,1:T(4,128)(2,1)} %copy.53), calls=%async_computation.3 | async-start | bytes 2621440 | tf_op jit(solution)/shard_map/all_to_all | solution.py:41
Sparse Core Ops, SparseCore 0:
  14.4 132.4 all-gather.1
where the time goes:
time: 382 us; the launch traced here: 375 us
  matrix products  188 us (49%)
  waiting for transfers between devices  45.3 us (12%)
  other arithmetic  38.5 us (10%)
  local copies, waits for them, and re-layouts  38.2 us (10%)
  blocking collectives  38 us (10%)
  between operations  14.5 us (4%)
  starting transfers between devices  12.7 us (3%)
    dot_general x2, matrix products, spectral_filter(): jnp.dot(field.reshape(count * rows * level_count, lon), table, preferred_...  66.5 us
    dot_general x2, matrix products, spectral_filter(): jnp.dot(returned.reshape(count * rows * level_count, width), table.T, pre...  62.8 us
    dot_general x2, matrix products, spectral_filter(): jnp.einsum('mln,bmnep->blemp', weighted_polynomial_basis, spectra, prefer...  58.9 us
    all_to_all x1, blocking collectives, spectral_filter(): lax.all_to_all(coeffs, 'lat', split_axis=3, concat_axis=1, tiled=True)  38 us
    all_to_all x1, waiting for transfers between devices, spectral_filter(): lax.all_to_all(coeffs, 'lat', split_axis=3, concat_axis=1, tiled=True)  28.6 us
    reduce_sum x1, other arithmetic, per_device(): jnp.sum(jnp.sign(local_realisation[None] - lax.all_gather(decoded_outlook...  26.1 us
    all_gather x1, waiting for transfers between devices, per_device(): lax.all_gather(decoded_outlook_array, 'member', axis=0, tiled=True)  16.7 us
    unnamed x8, local copies, waits for them, and re-layouts  8.49 us
  transfers between devices with their start and end apart: 4, of which 2 were waited for; matrix products, arithmetic and copies ran while one was open for 50% of the time, Pallas kernels for 0%

commit v1 on v0

v1 whole, which is shorter than its diff:
```python
import math

import jax
import jax.numpy as jnp
from jax import lax
from jax.experimental import pallas as pl
from jax.experimental.pallas import tpu as pltpu
from jax.sharding import PartitionSpec as P


def wave_trig(wave, place, lon):
    phase = (wave * place % lon).astype(jnp.float32) * (2.0 * math.pi / lon)
    return jnp.cos(phase), jnp.sin(phase)


def fourier_rows(lon, lat, member, per, waves):
    fine = math.gcd(lon, 128)
    row = lax.broadcasted_iota(jnp.int32, (lat.shape[0], per * 2, 1), 1)
    part = (row % 2).reshape(-1, 1)
    place = (member[:, None, None] * per + row // 2).reshape(-1, 1)
    wave = place + jnp.repeat(lat * waves, per * 2)[:, None]
    rows = wave.shape[0]
    scale = jnp.where(place < waves, math.sqrt(2.0 / lon), 0.0)
    cos_a, sin_a = wave_trig(wave, lax.broadcasted_iota(jnp.int32, (1, lon // fine), 1) * fine, lon)
    cos_b, sin_b = wave_trig(wave, lax.broadcasted_iota(jnp.int32, (1, fine), 1), lon)
    first = jnp.where(part == 0, cos_a, sin_a) * scale
    second = jnp.where(part == 0, -sin_a, cos_a) * scale
    first, second, cos_b, sin_b = lax.optimization_barrier((first, second, cos_b, sin_b))
    value = first[:, :, None] * cos_b[:, None, :] + second[:, :, None] * sin_b[:, None, :]
    return lax.optimization_barrier(value.reshape(rows, lon).astype(jnp.bfloat16))


def score_kernel(members, slots_ref, *refs):
    truth_ref, table_ref, out_ref, lines_ref = refs[members:]
    step, lon = truth_ref.shape
    padded = lines_ref.shape[0] // members
    inverse = 1.0 / (members - 1)
    lanes = 256 if lon % 256 == 0 else lon
    row = pl.program_id(0) * step
    one, minus, zero = (jnp.full((step, lanes), v, jnp.bfloat16) for v in (1, -1, 0))

    def sign(a, b):
        return jnp.where(a > b, one, jnp.where(a < b, minus, zero))

    def columns(c, carry):
        cols = pl.ds(pl.multiple_of(c * lanes, lanes), lanes)
        values = [refs[i][:, cols] for i in range(members)]
        truth = truth_ref[:, cols]
        ranks = [zero] * members
        for i in range(members):
            for j in range(i):
                s = sign(values[i], values[j])
                ranks[i] = ranks[i] + s
                ranks[j] = ranks[j] - s
        for i in range(members):
            grad = sign(values[i], truth).astype(jnp.float32)
            grad = grad - ranks[i].astype(jnp.float32) * inverse
            place = pl.multiple_of(slots_ref[i] * padded + row, 16)
            lines_ref[pl.ds(place, step), cols] = grad.astype(jnp.bfloat16)
        return carry

    lax.fori_loop(0, lon // lanes, columns, 0)

    @pl.when(pl.program_id(0) == pl.num_programs(0) - 1)
    def _():
        coeffs = lax.dot_general(
            table_ref[...],
            lines_ref[...],
            (((1,), (1,)), ((), ())),
            preferred_element_type=jnp.float32,
        )
        out_ref[...] = coeffs.astype(jnp.bfloat16)


def score_coeffs(blocks, slots, truth, table):
    members = len(blocks)
    piece, lon = truth.shape
    cols = table.shape[0]
    step = 16 if piece % 16 == 0 else piece
    padded = -(-piece // 16) * 16
    spec = pl.BlockSpec((step, lon), lambda i, s: (i, 0))
    coeffs = pl.pallas_call(
        lambda *refs: score_kernel(members, *refs),
        out_shape=jax.ShapeDtypeStruct((cols, members * padded), jnp.bfloat16),
        grid_spec=pltpu.PrefetchScalarGridSpec(
            num_scalar_prefetch=1,
            grid=(piece // step,),
            in_specs=[spec] * (members + 1) + [pl.BlockSpec((cols, lon), lambda i, s: (0, 0))],
            out_specs=pl.BlockSpec((cols, members * padded), lambda i, s: (0, 0)),
            scratch_shapes=[pltpu.VMEM((members * padded, lon), jnp.bfloat16)],
        ),
        compiler_params=pltpu.CompilerParams(vmem_limit_bytes=40 * 2**20),
        name="score",
    )(slots, *blocks, truth, table)
    coeffs = coeffs.reshape(cols, members, padded)[:, :, :piece]
    return coeffs.reshape(cols, members * piece)


def grid_kernel(rows, levels, coeffs_ref, table_ref, *refs):
    out_ref, lines_ref = refs[-2:]
    lines = rows * levels

    @pl.when(pl.program_id(0) == 0)
    def _():
        to = lax.broadcasted_iota(jnp.int32, (lines, lines), 0)
        at = lax.broadcasted_iota(jnp.int32, (lines, lines), 1)
        move = (to % levels * rows + to // levels == at).astype(jnp.bfloat16)
        moved = lax.dot_general(
            move, coeffs_ref[...], (((1,), (1,)), ((), ())), preferred_element_type=jnp.float32
        )
        lines_ref[...] = moved.astype(jnp.bfloat16)

    grid = jnp.dot(lines_ref[...], table_ref[...], preferred_element_type=jnp.float32)
    grid = grid.reshape(rows, levels, -1)
    if len(refs) == 3:
        grid = grid + refs[0][...].astype(jnp.float32)
    out_ref[...] = grid.astype(jnp.bfloat16)


def to_grid(coeffs, table, added, rows, levels):
    cols, lon = table.shape
    step = 512 if lon % 512 == 0 else lon
    block = pl.BlockSpec((rows, levels, step), lambda i: (0, 0, i))
    return pl.pallas_call(
        lambda *refs: grid_kernel(rows, levels, *refs),
        out_shape=jax.ShapeDtypeStruct((rows, levels, lon), jnp.bfloat16),
        grid=(lon // step,),
        in_specs=[
            pl.BlockSpec((cols, rows * levels), lambda i: (0, 0)),
            pl.BlockSpec((cols, step), lambda i: (0, i)),
        ]
        + [block] * (added is not None),
        out_specs=block,
        scratch_shapes=[pltpu.VMEM((rows * levels, cols), jnp.bfloat16)],
        name="grid",
    )(coeffs.reshape(cols, rows * levels), table, *([added] if added is not None else []))


def solution(mesh):
    members, lats = mesh.shape["member"], mesh.shape["lat"]
    both = ("lat", "member")

    def work(start, forcing, outlook, truth, basis, attenuation):
        _, rows, levels, lon = start.shape
        waves, lat_rows, _ = basis.shape
        per = -(-waves // members)
        halves = members // levels
        piece = rows // halves
        me = lax.axis_index("member")

        by_level = outlook[0].transpose(1, 0, 2).reshape(members, piece, lon)
        by_level = lax.optimization_barrier(by_level)
        sent = [lax.dynamic_index_in_dim(by_level, me ^ s, 0, False) for s in range(members)]
        sent, start = lax.optimization_barrier((sent, start))
        blocks, slots = [sent[0]], [me]
        for s in range(1, members):
            blocks.append(
                lax.ppermute(sent[s], "member", [(a, a ^ s) for a in range(members)])
            )
            slots.append(me ^ s)
        truth_here = lax.dynamic_slice(
            truth, (me % halves * piece, me // halves, 0), (piece, 1, lon)
        ).reshape(piece, lon)

        owner = jnp.arange(lats * members)
        table = fourier_rows(lon, owner // members, owner % members, per, waves)
        mine = jnp.pad(basis, ((0, members * per - waves), (0, 0), (0, 0)))
        mine = lax.dynamic_slice_in_dim(mine, me * per, per, 0)

        def lines_coeffs(lines):
            coeffs = lax.dot_general(
                table, lines, (((1,), (1,)), ((), ())), preferred_element_type=jnp.float32
            ).astype(jnp.bfloat16)
            return coeffs

        def to_waves(coeffs):
            coeffs = coeffs.reshape(lats * members, per // 2, 4, -1)
            return lax.all_to_all(coeffs, both, 0, 0, tiled=True)

        def legendre(coeffs):
            spectra = jnp.einsum(
                "jln,jcl->jcn", mine, coeffs, preferred_element_type=jnp.float32
            )
            spectra = (spectra * attenuation).astype(jnp.bfloat16)
            back = jnp.einsum(
                "jln,jcn->jcl", mine, spectra, preferred_element_type=jnp.float32
            ).astype(jnp.bfloat16)
            back = back.reshape(per, members, levels, 2, lats, rows)
            back = back.transpose(4, 1, 0, 3, 2, 5)
            return back.reshape(lats * members, per // 2, 4, levels * rows)

        lines = start[0].transpose(1, 0, 2).reshape(levels * rows, lon)
        received = to_waves(lines_coeffs(lines))
        score = score_coeffs(blocks, jnp.stack(slots), truth_here, table)
        received, score = lax.optimization_barrier((received, score))
        score = to_waves(score)
        coeffs = received.reshape(lats, members, per, 2, levels, rows)
        coeffs = coeffs.transpose(2, 1, 4, 3, 0, 5).reshape(per, members * levels * 2, lat_rows)
        state = to_waves(legendre(coeffs))

        coeffs = score.reshape(lats, levels, halves, per, 2, members, piece)
        coeffs = coeffs.transpose(3, 5, 1, 4, 0, 2, 6)
        coeffs = coeffs.reshape(per, members * levels * 2, lat_rows)
        score = to_waves(legendre(coeffs))
        advanced = to_grid(state, table, forcing[0], rows, levels)
        carried = to_grid(score, table, None, rows, levels)
        return advanced[None], carried[None]

    return jax.shard_map(
        work,
        mesh=mesh,
        in_specs=(
            P("member", "lat", None, None),
            P("member", "lat", None, None),
            P("member", "lat", None, None),
            P("lat", None, None),
            P("lat", None, None),
            P(),
        ),
        out_specs=(P("member", "lat", None, None), P("member", "lat", None, None)),
        check_vma=False,
    )
```

time: 382 us -> 176 us (0.46); the launches traced: 375 us -> 175 us
  matrix products: 188 us -> 14.8 us
  blocking collectives: 38 us -> 0 us
  other arithmetic: 38.5 us -> 4.35 us
  Pallas kernels: 0 us -> 25.5 us
  between operations: 14.5 us -> 0.99 us
  starting transfers between devices: 12.7 us -> 25.7 us
  waiting for transfers between devices: 45.3 us -> 57.3 us
  local copies, waits for them, and re-layouts: 38.2 us -> 46.2 us
    dot_general x6 -> x3, matrix products: 188 us -> 14.8 us  [the longest x2 11.1 us: legendre(): jnp.einsum('jln,jcn->jcl', mine, spectra, preferred_element_type=jnp.floa...]
    all_to_all x1 -> x0, blocking collectives: 38 us -> none  [spectral_filter(): lax.all_to_all(coeffs, 'lat', split_axis=3, concat_axis=1, tiled=True)]
    ppermute x0 -> x7, waiting for transfers between devices: none -> 32.6 us  [work(): lax.ppermute(sent[s], 'member', [(a, a ^ s) for a in range(members)])]
    reduce_sum x1 -> x0, other arithmetic: 26.1 us -> none  [per_device(): jnp.sum(jnp.sign(local_realisation[None] - lax.all_gather(decoded_outlook...]
    pallas_call x0 -> x3, Pallas kernels: none -> 25.5 us  [the longest x2 16.7 us: to_grid(): pl.pallas_call(lambda *refs: grid_kernel(rows, levels, *refs), out_shape=...]
    all_gather x1 -> x0, waiting for transfers between devices: 16.7 us -> none  [per_device(): lax.all_gather(decoded_outlook_array, 'member', axis=0, tiled=True)]
    convert_element_type x2 -> x1, other arithmetic: 12.4 us -> 2.63 us  [fourier_rows(): value.reshape(rows, lon).astype(jnp.bfloat16)]
    optimization_barrier x0 -> x3, local copies, waits for them, and re-layouts: none -> 7.46 us  [the longest x1 5.67 us: fourier_rows(): lax.optimization_barrier(value.reshape(rows, lon).astype(jnp.bfloat16))]
  transfers between devices with their start and end apart: 4 -> 11, of which waited for: 2 -> 8; matrix products, arithmetic and copies ran while one was open for 50% -> 21% of each run, Pallas kernels for 0% -> 10%
where the time goes in v1:
time: 176 us; the launch traced here: 175 us
  waiting for transfers between devices  57.3 us (33%)
  local copies, waits for them, and re-layouts  46.2 us (26%)
  starting transfers between devices  25.7 us (15%)
  Pallas kernels  25.5 us (14%)
  matrix products  14.8 us (8%)
  other arithmetic  4.35 us (2%)
    ppermute x7, waiting for transfers between devices, work(): lax.ppermute(sent[s], 'member', [(a, a ^ s) for a in range(members)])  32.6 us
    all_to_all x4, waiting for transfers between devices, to_waves(): return lax.all_to_all(coeffs, both, 0, 0, tiled=True)  24.7 us
    all_to_all x4, starting transfers between devices, to_waves(): return lax.all_to_all(coeffs, both, 0, 0, tiled=True)  19.4 us
    pallas_call x2, Pallas kernels, to_grid(): pl.pallas_call(lambda *refs: grid_kernel(rows, levels, *refs), out_shape=...  16.7 us
    dot_general x2, matrix products, legendre(): jnp.einsum('jln,jcn->jcl', mine, spectra, preferred_element_type=jnp.floa...  11.1 us
    unnamed x26, local copies, waits for them, and re-layouts  10.1 us
    pallas_call x1, Pallas kernels, score_coeffs(): pl.pallas_call(lambda *refs: score_kernel(members, *refs), out_shape=jax....  8.84 us
    ppermute x7, starting transfers between devices, work(): lax.ppermute(sent[s], 'member', [(a, a ^ s) for a in range(members)])  6.28 us
  transfers between devices with their start and end apart: 11, of which 8 were waited for; matrix products, arithmetic and copies ran while one was open for 21% of the time, Pallas kernels for 10%

profile of v1, /device:TPU:0, one launch (start us, length us, event | category | flops | bytes accessed | tf_op | source)
XLA Modules:
  0.0 174.8 jit_solution(4530605667244948224)
XLA Ops:
  1.4 1.3 fusion.36
  3.1 2.6 %add_convert_fusion = bf16[640,20,128]{0,2,1:T(8,128)(2,1)} fusion(f32[640,128]{0,1:T(8,128)S(1)} %get-tuple-element.20, f32[640,20]{0,1:T(8,128)S(1)} %get-tuple-element.19, f32[640,128]{0,1:T(8,128)S(1)} %get-tuple-element.18, f32[640,20]{0,1:T(8,128)S(1)} %get-tuple-element.17), kind=kLoop, calls=%fused_computation | loop fusion | flops 6553600 | bytes 4034560 | tf_op jit(solution)/shard_map/convert_element_type | solution.py:30
  5.7 2.3 %copy.30 = bf16[1,160,4,2560]{3,1,2,0:T(8,128)(2,1)} copy(bf16[1,160,4,2560]{3,2,1,0:T(4,128)(2,1)S(1)} %copy-done.9) | data formatting | bytes 6553600 | tf_op args[2]
  7.9 3.8 %dynamic-slice_bitcast_fusion = (bf16[80,2560]{1,0:T(8,128)(2,1)}, bf16[80,2560]{1,0:T(8,128)(2,1)}, bf16[80,2560]{1,0:T(8,128)(2,1)}, bf16[80,2560]{1,0:T(8,128...) fusion(bf16[8,80,2560]{2,1,0:T(8,128)(2,1)} %bitcast.64, ...), kind=kLoop, calls=%fused_computation.20 | loop fusion | bytes 6553632 | tf_op jit(solution)/shard_map/jit(dynamic_index_in_dim)/squeeze | solution.py:153
  12.3 1.4 copy-done.8
  13.7 3.6 %convolution_convert_fusion = bf16[640,640]{1,0:T(8,128)(2,1)} fusion(bf16[640,2560]{0,1:T(8,128)(2,1)S(1)} %bitcast.63, bf16[640,2560]{1,0:T(8,128)(2,1)S(1)} %bitcast.70), kind=kOutput, calls=%fused_computation.11 | convolution fusion | flops 2097561600 | bytes 7372800 | tf_op jit(solution)/shard_map/dot_general | solution.py:171
  17.3 2.4 %reshape.215 = bf16[32,5,4,640]{3,2,1,0:T(4,128)(2,1)} reshape(bf16[640,640]{1,0:T(8,128)(2,1)} %convolution_convert_fusion) | data formatting | bytes 1638400 | tf_op jit(solution)/shard_map/reshape | solution.py:177
  19.7 7.4 %all-to-all-start = ((bf16[32,5,4,640]{3,2,1,0:T(4,128)(2,1)}), bf16[32,5,4,640]{3,2,1,0:T(4,128)(2,1)}, u32[]{:S(2)}, u32[]{:S(2)}) async-start(bf16[32,5,4,640]{3,2,1,0:T(4,128)(2,1)} %reshape.215), calls=%async_computation | async-start | bytes 1638400 | tf_op jit(solution)/shard_map/all_to_all | solution.py:178
  27.4 1.6 collective-permute-start.1
  29.1 1.7 collective-permute-start.3
  30.9 0.8 copy-done.4
  31.7 2.5 %collective-permute-start.5 = (bf16[80,2560]{1,0:T(8,128)(2,1)}, bf16[80,2560]{1,0:T(8,128)(2,1)}, u32[]{:S(2)}, u32[]{:S(2)}) collective-permute-start(bf16[80,2560]{1,0:T(8,128)(2,1)} %get-tuple-element.28), channel_id=1, source_target_pairs={{0,24},{4,28},{8,16},{12,20},{16,8},{20,12},{24,0},{28,4},{1,25},{... | collective-permute-start | bytes 1228808 | tf_op jit(solution)/shard_map/ppermute | solution.py:158
  34.2 13.6 %collective-permute-done.1.refs_3_ = bf16[80,2560]{1,0:T(8,128)(2,1)S(1)} collective-permute-done((bf16[80,2560]{1,0:T(8,128)(2,1)}, bf16[80,2560]{1,0:T(8,128)(2,1)S(1)}, u32[]{:S(2)}, u32[]{:S(2)}) %collective-permute-start.1) | collective-permute-done | bytes 409632 | tf_op jit(solution)/shard_map/ppermute | solution.py:158
  47.8 0.7 copy-done.6
  48.6 5.7 %copy.33.refs_10_.refs_1_ = bf16[640,2560]{1,0:T(8,128)(2,1)} copy(bf16[640,2560]{0,1:T(8,128)(2,1)} %bitcast.62) | data formatting | bytes 6553600 | tf_op jit(solution)/shard_map/optimization_barrier | solution.py:30
  54.3 0.8 constant_dynamic-slice_fusion
  56.0 10.5 %collective-permute-done.5.refs_7_ = bf16[80,2560]{1,0:T(8,128)(2,1)} collective-permute-done((bf16[80,2560]{1,0:T(8,128)(2,1)}, bf16[80,2560]{1,0:T(8,128)(2,1)}, u32[]{:S(2)}, u32[]{:S(2)}) %collective-permute-start.5) | collective-permute-done | bytes 409632 | tf_op jit(solution)/shard_map/ppermute | solution.py:158
  66.6 7.6 %collective-permute-done.6.refs_8_ = bf16[80,2560]{1,0:T(8,128)(2,1)} collective-permute-done((bf16[80,2560]{1,0:T(8,128)(2,1)}, bf16[80,2560]{1,0:T(8,128)(2,1)}, u32[]{:S(2)}, u32[]{:S(2)}) %collective-permute-start.6) | collective-permute-done | bytes 409632 | tf_op jit(solution)/shard_map/ppermute | solution.py:158
  74.2 1.9 %copy-done.2 = bf16[640,2560]{1,0:T(8,128)(2,1)S(1)} copy-done((bf16[640,2560]{1,0:T(8,128)(2,1)S(1)}, bf16[640,2560]{1,0:T(8,128)(2,1)}, u32[]{:S(2)}) %copy-start.2) | copy-done | bytes 3276824
  76.1 1.0 copy-done.3
  77.1 1.0 copy-done.5
  78.1 1.0 copy-done.7
  79.1 8.8 %score.1 = bf16[640,640]{1,0:T(8,128)(2,1)S(1)} custom-call(s32[8]{0:T(128)S(1)} %stack.35.refs_0_, bf16[80,2560]{1,0:T(8,128)(2,1)S(1)} %copy-done.3, bf16[80,2560]{1,0:T(8,128)(2,1)S(1)} %copy-done.5, bf16[80,2560]{1,0:T(8,128)(2,1)S(1)} %copy-done.7, bf16[80,2560]{1,0:T(8,128)(2,1)} %collective-permute-done.2.refs_4_, ...), custom_call_target="tpu_custom_call" | custom-call | tf_op jit(solution)/shard_map/score/pallas_call | solution.py:82
  88.0 1.1 reshape.222
  89.1 4.3 %all-to-all-start.2 = ((bf16[32,5,4,640]{3,2,1,0:T(4,128)(2,1)}), bf16[32,5,4,640]{3,2,1,0:T(4,128)(2,1)}, u32[]{:S(2)}, u32[]{:S(2)}) async-start(bf16[32,5,4,640]{3,2,1,0:T(4,128)(2,1)} %reshape.222), calls=%async_computation.2 | async-start | bytes 1638400 | tf_op jit(solution)/shard_map/all_to_all | solution.py:178
  93.3 1.2 copy.34
  94.6 0.9 reshape.217
  95.5 1.7 copy.35
  97.2 0.8 reshape.218
  98.1 5.6 %fusion.8 = bf16[10,64,640]{2,1,0:T(8,128)(2,1)S(1)} fusion(bf16[80,640,320]{1,2,0:T(8,128)(2,1)} %param.10, s32[]{:T(128)S(6)} %select_n.175, bf16[10,64,640]{2,1,0:T(8,128)(2,1)S(1)} %reshape.218, f32[320]{0:T(512)S(1)} %copy-done.11), kind=kOutput, calls=%fused_computation.9 | convolution fusion | flops 525107200 | bytes 9832704 | tf_op jit(solution)/shard_map/jln,jcn->jcl/dot_general | solution.py:185
  103.6 0.9 reshape.219
  105.1 1.9 %reshape.220 = bf16[32,5,4,640]{3,2,1,0:T(4,128)(2,1)} reshape(bf16[4,8,10,2,4,160]{5,4,3,2,1,0:T(4,128)(2,1)S(1)} %copy.36) | data formatting | bytes 1638400 | tf_op jit(solution)/shard_map/reshape | solution.py:190
  107.0 7.4 %all-to-all-done.2 = bf16[32,5,4,640]{3,2,1,0:T(4,128)(2,1)} async-done(((bf16[32,5,4,640]{3,2,1,0:T(4,128)(2,1)}), bf16[32,5,4,640]{3,2,1,0:T(4,128)(2,1)}, u32[]{:S(2)}, u32[]{:S(2)}) %all-to-all-start.2) | async-done | bytes 819232 | tf_op jit(solution)/shard_map/all_to_all | solution.py:178
  114.4 3.7 %all-to-all-start.1 = ((bf16[32,5,4,640]{3,2,1,0:T(4,128)(2,1)}), bf16[32,5,4,640]{3,2,1,0:T(4,128)(2,1)}, u32[]{:S(2)}, u32[]{:S(2)}) async-start(bf16[32,5,4,640]{3,2,1,0:T(4,128)(2,1)} %reshape.220), calls=%async_computation.1 | async-start | bytes 1638400 | tf_op jit(solution)/shard_map/all_to_all | solution.py:178
  118.2 1.2 copy.38
  119.4 1.4 reshape.223
  120.8 1.4 copy.39
  122.2 1.0 reshape.224
  123.2 5.6 %fusion.11 = bf16[10,64,640]{2,1,0:T(8,128)(2,1)S(1)} fusion(bf16[80,640,320]{1,2,0:T(8,128)(2,1)} %param.10, s32[]{:T(128)S(6)} %select_n.175, bf16[10,64,640]{2,1,0:T(8,128)(2,1)S(1)} %reshape.224, f32[320]{0:T(512)S(1)} %copy-done.11), kind=kOutput, calls=%fused_computation.10 | convolution fusion | flops 525107200 | bytes 9832704 | tf_op jit(solution)/shard_map/jln,jcn->jcl/dot_general | solution.py:185
  128.8 0.9 reshape.225
  130.2 1.9 %reshape.226 = bf16[32,5,4,640]{3,2,1,0:T(4,128)(2,1)} reshape(bf16[4,8,10,2,4,160]{5,4,3,2,1,0:T(4,128)(2,1)S(1)} %copy.40) | data formatting | bytes 1638400 | tf_op jit(solution)/shard_map/reshape | solution.py:190
  132.1 7.3 %all-to-all-done.1 = bf16[32,5,4,640]{3,2,1,0:T(4,128)(2,1)} async-done(((bf16[32,5,4,640]{3,2,1,0:T(4,128)(2,1)}), bf16[32,5,4,640]{3,2,1,0:T(4,128)(2,1)}, u32[]{:S(2)}, u32[]{:S(2)}) %all-to-all-start.1) | async-done | bytes 819232 | tf_op jit(solution)/shard_map/all_to_all | solution.py:178
  139.4 4.0 %all-to-all-start.3 = ((bf16[32,5,4,640]{3,2,1,0:T(4,128)(2,1)}), bf16[32,5,4,640]{3,2,1,0:T(4,128)(2,1)}, u32[]{:S(2)}, u32[]{:S(2)}) async-start(bf16[32,5,4,640]{3,2,1,0:T(4,128)(2,1)} %reshape.226), calls=%async_computation.3 | async-start | bytes 1638400 | tf_op jit(solution)/shard_map/all_to_all | solution.py:178
  143.4 2.3 %reshape.221.refs_0_ = bf16[640,640]{1,0:T(8,128)(2,1)} reshape(bf16[32,5,4,640]{3,2,1,0:T(4,128)(2,1)} %all-to-all-done.1) | data formatting | bytes 1638400 | tf_op jit(solution)/shard_map/reshape | solution.py:136
  145.7 8.8 %grid.2 = bf16[160,4,2560]{2,1,0:T(4,128)(2,1)} custom-call(bf16[640,640]{1,0:T(8,128)(2,1)} %reshape.221.refs_0_, bf16[640,2560]{1,0:T(8,128)(2,1)} %copy.33.refs_10_.refs_1_, bf16[160,4,2560]{2,1,0:T(4,128)(2,1)} %bitcast.71), custom_call_target="tpu_custom_call" | custom-call | tf_op jit(solution)/shard_map/grid/pallas_call | solution.py:124
  154.5 10.0 %all-to-all-done.3 = bf16[32,5,4,640]{3,2,1,0:T(4,128)(2,1)} async-done(((bf16[32,5,4,640]{3,2,1,0:T(4,128)(2,1)}), bf16[32,5,4,640]{3,2,1,0:T(4,128)(2,1)}, u32[]{:S(2)}, u32[]{:S(2)}) %all-to-all-start.3) | async-done | bytes 819232 | tf_op jit(solution)/shard_map/all_to_all | solution.py:178
  164.5 2.4 %reshape.227.refs_0_ = bf16[640,640]{1,0:T(8,128)(2,1)} reshape(bf16[32,5,4,640]{3,2,1,0:T(4,128)(2,1)} %all-to-all-done.3) | data formatting | bytes 1638400 | tf_op jit(solution)/shard_map/reshape | solution.py:136
  166.9 7.9 %grid.3 = bf16[160,4,2560]{2,1,0:T(4,128)(2,1)} custom-call(bf16[640,640]{1,0:T(8,128)(2,1)} %reshape.227.refs_0_, bf16[640,2560]{1,0:T(8,128)(2,1)} %copy.33.refs_10_.refs_1_), custom_call_target="tpu_custom_call" | custom-call | tf_op jit(solution)/shard_map/grid/pallas_call | solution.py:124
  (47 shorter events, 3.9 us)
Async XLA Ops:
  0.6 53.6 %copy-start = (bf16[160,4,2560]{2,1,0:T(4,128)(2,1)S(1)}, bf16[160,4,2560]{2,1,0:T(4,128)(2,1)}, u32[]{:S(2)}) copy-start(bf16[160,4,2560]{2,1,0:T(4,128)(2,1)} %param.9) | copy-start | bytes 9830404
  1.4 4.3 %copy-start.9 = (bf16[1,160,4,2560]{3,2,1,0:T(4,128)(2,1)S(1)}, bf16[1,160,4,2560]{3,2,1,0:T(4,128)(2,1)}, u32[]{:S(2)}) copy-start(bf16[1,160,4,2560]{3,2,1,0:T(4,128)(2,1)} %param.8) | copy-start | bytes 9830404
  7.9 3.8 %copy-start.10 = (bf16[1,160,4,2560]{3,2,1,0:T(4,128)(2,1)S(1)}, bf16[1,160,4,2560]{3,2,1,0:T(4,128)(2,1)}, u32[]{:S(2)}) copy-start(bf16[1,160,4,2560]{3,2,1,0:T(4,128)(2,1)} %param.6) | copy-start | bytes 9830404
  11.7 1.9 %copy-start.8 = (bf16[640,20,128]{0,2,1:T(8,128)(2,1)S(1)}, bf16[640,20,128]{0,2,1:T(8,128)(2,1)}, u32[]{:S(2)}) copy-start(bf16[640,20,128]{0,2,1:T(8,128)(2,1)} %add_convert_fusion) | copy-start | bytes 9830404
  19.7 68.3 %all-to-all-start = ((bf16[32,5,4,640]{3,2,1,0:T(4,128)(2,1)}), bf16[32,5,4,640]{3,2,1,0:T(4,128)(2,1)}, u32[]{:S(2)}, u32[]{:S(2)}) async-start(bf16[32,5,4,640]{3,2,1,0:T(4,128)(2,1)} %reshape.215), calls=%async_computation | async-start | bytes 1638400 | tf_op jit(solution)/shard_map/all_to_all | solution.py:178
  27.2 3.7 %collective-permute-start = (bf16[80,2560]{1,0:T(8,128)(2,1)}, bf16[80,2560]{1,0:T(8,128)(2,1)S(1)}, u32[]{:S(2)}, u32[]{:S(2)}) collective-permute-start(bf16[80,2560]{1,0:T(8,128)(2,1)} %get-tuple-element.23), channel_id=1, source_target_pairs={{0,4},{4,0},{8,12},{12,8},{16,20},{20,16},{24,28},{28,24},{1,5},{5... | collective-permute-start | bytes 1228808 | tf_op jit(solution)/shard_map/ppermute | solution.py:158
  27.4 20.4 %collective-permute-start.1 = (bf16[80,2560]{1,0:T(8,128)(2,1)}, bf16[80,2560]{1,0:T(8,128)(2,1)S(1)}, u32[]{:S(2)}, u32[]{:S(2)}) collective-permute-start(bf16[80,2560]{1,0:T(8,128)(2,1)} %get-tuple-element.24), channel_id=1, source_target_pairs={{0,8},{4,12},{8,0},{12,4},{16,24},{20,28},{24,16},{28,20},{1,9},{5... | collective-permute-start | bytes 1228808 | tf_op jit(solution)/shard_map/ppermute | solution.py:158
  29.0 26.7 %collective-permute-start.2 = (bf16[80,2560]{1,0:T(8,128)(2,1)}, bf16[80,2560]{1,0:T(8,128)(2,1)}, u32[]{:S(2)}, u32[]{:S(2)}) collective-permute-start(bf16[80,2560]{1,0:T(8,128)(2,1)} %get-tuple-element.25), channel_id=1, source_target_pairs={{0,12},{4,8},{8,4},{12,0},{16,28},{20,24},{24,20},{28,16},{1,13},{... | collective-permute-start | bytes 1228808 | tf_op jit(solution)/shard_map/ppermute | solution.py:158
  29.1 26.6 %collective-permute-start.3 = (bf16[80,2560]{1,0:T(8,128)(2,1)}, bf16[80,2560]{1,0:T(8,128)(2,1)}, u32[]{:S(2)}, u32[]{:S(2)}) collective-permute-start(bf16[80,2560]{1,0:T(8,128)(2,1)} %get-tuple-element.26), channel_id=1, source_target_pairs={{0,16},{4,20},{8,24},{12,28},{16,0},{20,4},{24,8},{28,12},{1,17},{... | collective-permute-start | bytes 1228808 | tf_op jit(solution)/shard_map/ppermute | solution.py:158
  30.8 25.3 %collective-permute-start.4 = (bf16[80,2560]{1,0:T(8,128)(2,1)}, bf16[80,2560]{1,0:T(8,128)(2,1)}, u32[]{:S(2)}, u32[]{:S(2)}) collective-permute-start(bf16[80,2560]{1,0:T(8,128)(2,1)} %get-tuple-element.27), channel_id=1, source_target_pairs={{0,20},{4,16},{8,28},{12,24},{16,4},{20,0},{24,12},{28,8},{1,21},{... | collective-permute-start | bytes 1228808 | tf_op jit(solution)/shard_map/ppermute | solution.py:158
  30.9 0.8 copy-start.4
  31.7 34.9 %collective-permute-start.5 = (bf16[80,2560]{1,0:T(8,128)(2,1)}, bf16[80,2560]{1,0:T(8,128)(2,1)}, u32[]{:S(2)}, u32[]{:S(2)}) collective-permute-start(bf16[80,2560]{1,0:T(8,128)(2,1)} %get-tuple-element.28), channel_id=1, source_target_pairs={{0,24},{4,28},{8,16},{12,20},{16,8},{20,12},{24,0},{28,4},{1,25},{... | collective-permute-start | bytes 1228808 | tf_op jit(solution)/shard_map/ppermute | solution.py:158
  47.8 0.7 copy-start.6
  48.6 25.6 %collective-permute-start.6 = (bf16[80,2560]{1,0:T(8,128)(2,1)}, bf16[80,2560]{1,0:T(8,128)(2,1)}, u32[]{:S(2)}, u32[]{:S(2)}) collective-permute-start(bf16[80,2560]{1,0:T(8,128)(2,1)} %get-tuple-element.29), channel_id=1, source_target_pairs={{0,28},{4,24},{8,20},{12,16},{16,12},{20,8},{24,4},{28,0},{1,29},{... | collective-permute-start | bytes 1228808 | tf_op jit(solution)/shard_map/ppermute | solution.py:158
  74.2 1.9 %copy-start.2 = (bf16[640,2560]{1,0:T(8,128)(2,1)S(1)}, bf16[640,2560]{1,0:T(8,128)(2,1)}, u32[]{:S(2)}) copy-start(bf16[640,2560]{1,0:T(8,128)(2,1)} %copy.33.refs_10_.refs_1_) | copy-start | bytes 9830404
  76.1 1.0 copy-start.3
  77.1 1.0 copy-start.5
  78.1 1.0 copy-start.7
  89.1 25.4 %all-to-all-start.2 = ((bf16[32,5,4,640]{3,2,1,0:T(4,128)(2,1)}), bf16[32,5,4,640]{3,2,1,0:T(4,128)(2,1)}, u32[]{:S(2)}, u32[]{:S(2)}) async-start(bf16[32,5,4,640]{3,2,1,0:T(4,128)(2,1)} %reshape.222), calls=%async_computation.2 | async-start | bytes 1638400 | tf_op jit(solution)/shard_map/all_to_all | solution.py:178
  94.6 3.5 %copy-start.11 = (f32[320]{0:T(512)S(1)}, f32[320]{0:T(512)}, u32[]{:S(2)}) copy-start(f32[320]{0:T(512)} %param.11) | copy-start | bytes 3844
  114.4 25.0 %all-to-all-start.1 = ((bf16[32,5,4,640]{3,2,1,0:T(4,128)(2,1)}), bf16[32,5,4,640]{3,2,1,0:T(4,128)(2,1)}, u32[]{:S(2)}, u32[]{:S(2)}) async-start(bf16[32,5,4,640]{3,2,1,0:T(4,128)(2,1)} %reshape.220), calls=%async_computation.1 | async-start | bytes 1638400 | tf_op jit(solution)/shard_map/all_to_all | solution.py:178
  139.4 25.0 %all-to-all-start.3 = ((bf16[32,5,4,640]{3,2,1,0:T(4,128)(2,1)}), bf16[32,5,4,640]{3,2,1,0:T(4,128)(2,1)}, u32[]{:S(2)}, u32[]{:S(2)}) async-start(bf16[32,5,4,640]{3,2,1,0:T(4,128)(2,1)} %reshape.226), calls=%async_computation.3 | async-start | bytes 1638400 | tf_op jit(solution)/shard_map/all_to_all | solution.py:178
  164.5 10.4 %copy-start.1 = (bf16[160,4,2560]{2,1,0:T(4,128)(2,1)S(1)}, bf16[160,4,2560]{2,1,0:T(4,128)(2,1)}, u32[]{:S(2)}) copy-start(bf16[160,4,2560]{2,1,0:T(4,128)(2,1)} %param.9) | copy-start | bytes 9830404

commit v2 on v1

--- a/solution.py
+++ b/solution.py
@@ -30,8 +30,50 @@
     return lax.optimization_barrier(value.reshape(rows, lon).astype(jnp.bfloat16))
 
 
+def split_kernel(halves, me_ref, *refs):
+    ins, outs, pieces_ref = refs[:halves], refs[halves:-1], refs[-1]
+    step, levels, lon = ins[0].shape
+    lines = step * levels
+    to = lax.broadcasted_iota(jnp.int32, (lines, lines), 0)
+    at = lax.broadcasted_iota(jnp.int32, (lines, lines), 1)
+    move = (to % step * levels + to // step == at).astype(jnp.bfloat16)
+    for h in range(halves):
+        moved = jnp.dot(
+            move, ins[h][...].reshape(lines, lon), preferred_element_type=jnp.float32
+        ).astype(jnp.bfloat16)
+        for e in range(levels):
+            pieces_ref[e * halves + h] = moved[e * step : (e + 1) * step]
+    for s, out_ref in enumerate(outs):
+        out_ref[...] = pieces_ref[me_ref[0] ^ s]
+
+
+def split(field, me, members):
+    rows, levels, lon = field.shape
+    halves = members // levels
+    piece = rows // halves
+    step = 16 if piece % 16 == 0 else piece
+    blocks = piece // step
+    return pl.pallas_call(
+        lambda *refs: split_kernel(halves, *refs),
+        out_shape=[jax.ShapeDtypeStruct((piece, lon), jnp.bfloat16)] * members,
+        grid_spec=pltpu.PrefetchScalarGridSpec(
+            num_scalar_prefetch=1,
+            grid=(blocks,),
+            in_specs=[
+                pl.BlockSpec((step, levels, lon), lambda i, s, h=h: (h * blocks + i, 0, 0))
+                for h in range(halves)
+            ],
+            out_specs=[pl.BlockSpec((step, lon), lambda i, s: (i, 0))] * members,
+            scratch_shapes=[pltpu.VMEM((members, step, lon), jnp.bfloat16)],
+        ),
+        name="split",
+    )(me.reshape(1), *[field] * halves)
+
+
 def score_kernel(members, slots_ref, *refs):
-    truth_ref, table_ref, out_ref, lines_ref = refs[members:]
+    truth_ref, table_hbm, out_ref, lines_ref, table_ref, arrived = refs[members:]
+    copy = pltpu.make_async_copy(table_hbm, table_ref, arrived)
+    pl.when(pl.program_id(0) == 0)(copy.start)
     step, lon = truth_ref.shape
     padded = lines_ref.shape[0] // members
     inverse = 1.0 / (members - 1)
@@ -63,13 +105,14 @@
 
     @pl.when(pl.program_id(0) == pl.num_programs(0) - 1)
     def _():
+        copy.wait()
         coeffs = lax.dot_general(
             table_ref[...],
             lines_ref[...],
             (((1,), (1,)), ((), ())),
             preferred_element_type=jnp.float32,
         )
-        out_ref[...] = coeffs.astype(jnp.bfloat16)
+        out_ref[...] = coeffs.reshape(out_ref.shape).astype(jnp.bfloat16)
 
 
 def score_coeffs(blocks, slots, truth, table):
@@ -81,19 +124,23 @@
     spec = pl.BlockSpec((step, lon), lambda i, s: (i, 0))
     coeffs = pl.pallas_call(
         lambda *refs: score_kernel(members, *refs),
-        out_shape=jax.ShapeDtypeStruct((cols, members * padded), jnp.bfloat16),
+        out_shape=jax.ShapeDtypeStruct((cols // 4, 4, members * padded), jnp.bfloat16),
         grid_spec=pltpu.PrefetchScalarGridSpec(
             num_scalar_prefetch=1,
             grid=(piece // step,),
-            in_specs=[spec] * (members + 1) + [pl.BlockSpec((cols, lon), lambda i, s: (0, 0))],
-            out_specs=pl.BlockSpec((cols, members * padded), lambda i, s: (0, 0)),
-            scratch_shapes=[pltpu.VMEM((members * padded, lon), jnp.bfloat16)],
+            in_specs=[spec] * (members + 1) + [pl.BlockSpec(memory_space=pltpu.HBM)],
+            out_specs=pl.BlockSpec((cols // 4, 4, members * padded), lambda i, s: (0, 0, 0)),
+            scratch_shapes=[
+                pltpu.VMEM((members * padded, lon), jnp.bfloat16),
+                pltpu.VMEM((cols, lon), jnp.bfloat16),
+                pltpu.SemaphoreType.DMA,
+            ],
         ),
-        compiler_params=pltpu.CompilerParams(vmem_limit_bytes=40 * 2**20),
+        compiler_params=pltpu.CompilerParams(vmem_limit_bytes=60 * 2**20),
         name="score",
     )(slots, *blocks, truth, table)
-    coeffs = coeffs.reshape(cols, members, padded)[:, :, :piece]
-    return coeffs.reshape(cols, members * piece)
+    coeffs = coeffs.reshape(cols // 4, 4, members, padded)[..., :piece]
+    return coeffs.reshape(cols // 4, 4, members * piece)
 
 
 def grid_kernel(rows, levels, coeffs_ref, table_ref, *refs):
@@ -106,7 +153,10 @@
         at = lax.broadcasted_iota(jnp.int32, (lines, lines), 1)
         move = (to % levels * rows + to // levels == at).astype(jnp.bfloat16)
         moved = lax.dot_general(
-            move, coeffs_ref[...], (((1,), (1,)), ((), ())), preferred_element_type=jnp.float32
+            move,
+            coeffs_ref[...].reshape(-1, lines),
+            (((1,), (1,)), ((), ())),
+            preferred_element_type=jnp.float32,
         )
         lines_ref[...] = moved.astype(jnp.bfloat16)
 
@@ -126,14 +176,14 @@
         out_shape=jax.ShapeDtypeStruct((rows, levels, lon), jnp.bfloat16),
         grid=(lon // step,),
         in_specs=[
-            pl.BlockSpec((cols, rows * levels), lambda i: (0, 0)),
+            pl.BlockSpec((cols // 4, 4, rows * levels), lambda i: (0, 0, 0)),
             pl.BlockSpec((cols, step), lambda i: (0, i)),
         ]
         + [block] * (added is not None),
         out_specs=block,
         scratch_shapes=[pltpu.VMEM((rows * levels, cols), jnp.bfloat16)],
         name="grid",
-    )(coeffs.reshape(cols, rows * levels), table, *([added] if added is not None else []))
+    )(coeffs.reshape(cols // 4, 4, rows * levels), table, *([added] if added is not None else []))
 
 
 def solution(mesh):
@@ -148,9 +198,7 @@
         piece = rows // halves
         me = lax.axis_index("member")
 
-        by_level = outlook[0].transpose(1, 0, 2).reshape(members, piece, lon)
-        by_level = lax.optimization_barrier(by_level)
-        sent = [lax.dynamic_index_in_dim(by_level, me ^ s, 0, False) for s in range(members)]
+        sent = split(outlook[0], me, members)
         sent, start = lax.optimization_barrier((sent, start))
         blocks, slots = [sent[0]], [me]
         for s in range(1, members):

time: 176 us -> 170 us (0.966)
  local copies, waits for them, and re-layouts: 46.2 us -> 30.1 us
  Pallas kernels: 25.5 us -> 33 us
  waiting for transfers between devices: 57.3 us -> 59.9 us
    unnamed x26 -> x9, local copies, waits for them, and re-layouts: 10.1 us -> 1.1 us
    pallas_call x0 -> x1, Pallas kernels: none -> 5.66 us  [split(): pl.pallas_call(lambda *refs: split_kernel(halves, *refs), out_shape=[jax....]
    reshape x2 -> x0, local copies, waits for them, and re-layouts: 4.73 us -> none  [to_grid(): coeffs.reshape(cols, rows * levels)]
    squeeze x1 -> x0, local copies, waits for them, and re-layouts: 3.79 us -> none  [work(): lax.dynamic_index_in_dim(by_level, me ^ s, 0, False)]
    all_to_all x4, waiting for transfers between devices: 24.7 us -> 27 us  [to_waves(): return lax.all_to_all(coeffs, both, 0, 0, tiled=True)]
    optimization_barrier x1, local copies, waits for them, and re-layouts: 0.55 us -> 2.62 us  [work(): sent, start = lax.optimization_barrier((sent, start))]
  transfers between devices with their start and end apart: 11 -> 11, of which waited for: 8 -> 7; matrix products, arithmetic and copies ran while one was open for 21% -> 21% of each run, Pallas kernels for 10% -> 11%
where the time goes in v2:
time: 170 us; the launch traced here: 169 us
  waiting for transfers between devices  59.9 us (35%)
  Pallas kernels  33 us (19%)
  local copies, waits for them, and re-layouts  30.1 us (18%)
  starting transfers between devices  25.7 us (15%)
  matrix products  14.8 us (9%)
  other arithmetic  4.35 us (3%)
    ppermute x7, waiting for transfers between devices, work(): lax.ppermute(sent[s], 'member', [(a, a ^ s) for a in range(members)])  32.9 us
    all_to_all x4, waiting for transfers between devices, to_waves(): return lax.all_to_all(coeffs, both, 0, 0, tiled=True)  27 us
    all_to_all x4, starting transfers between devices, to_waves(): return lax.all_to_all(coeffs, both, 0, 0, tiled=True)  19.4 us
    pallas_call x2, Pallas kernels, to_grid(): pl.pallas_call(lambda *refs: grid_kernel(rows, levels, *refs), out_shape=...  16.9 us
    dot_general x2, matrix products, legendre(): jnp.einsum('jln,jcn->jcl', mine, spectra, preferred_element_type=jnp.floa...  11.1 us
    pallas_call x1, Pallas kernels, score_coeffs(): pl.pallas_call(lambda *refs: score_kernel(members, *refs), out_shape=jax....  10.5 us
    ppermute x7, starting transfers between devices, work(): lax.ppermute(sent[s], 'member', [(a, a ^ s) for a in range(members)])  6.28 us
    pallas_call x1, Pallas kernels, split(): pl.pallas_call(lambda *refs: split_kernel(halves, *refs), out_shape=[jax....  5.66 us
  transfers between devices with their start and end apart: 11, of which 7 were waited for; matrix products, arithmetic and copies ran while one was open for 21% of the time, Pallas kernels for 11%

profile of v2, /device:TPU:0, one launch (start us, length us, event | category | flops | bytes accessed | tf_op | source)
XLA Modules:
  0.0 168.8 jit_solution(5788969520124663069)
XLA Ops:
  1.2 0.1 eq.27
  1.3 1.3 fusion.36
  2.7 0.3 select_multiply_fusion
  3.0 2.6 %add_convert_fusion = bf16[640,20,128]{0,2,1:T(8,128)(2,1)} fusion(f32[640,128]{0,1:T(8,128)S(1)} %get-tuple-element.28, f32[640,20]{0,1:T(8,128)S(1)} %get-tuple-element.27, f32[640,128]{0,1:T(8,128)S(1)} %get-tuple-element.26, f32[640,20]{0,1:T(8,128)S(1)} %get-tuple-element.25), kind=kLoop, calls=%fused_computation | loop fusion | flops 6553600 | bytes 4034560 | tf_op jit(solution)/shard_map/convert_element_type | solution.py:30
  5.6 5.7 %split.1 = (bf16[80,2560]{1,0:T(8,128)(2,1)}, bf16[80,2560]{1,0:T(8,128)(2,1)}, bf16[80,2560]{1,0:T(8,128)(2,1)}, bf16[80,2560]{1,0:T(8,128)(2,1)}, bf16[80,2560...) custom-call(s32[1]{0:T(128)} %bitcast.1.refs_0_, ...), custom_call_target="tpu_custom_call" | custom-call | tf_op jit(solution)/shard_map/split/pallas_call | solution.py:56
  11.3 2.6 %copy.28 = bf16[1,160,4,2560]{3,1,2,0:T(8,128)(2,1)S(1)} copy(bf16[1,160,4,2560]{3,2,1,0:T(4,128)(2,1)} %param.6) | data formatting | bytes 6553600 | tf_op jit(solution)/shard_map/optimization_barrier | solution.py:202
  13.9 0.3 copy-done.2
  14.2 3.6 %convolution_convert_fusion = bf16[640,640]{1,0:T(8,128)(2,1)} fusion(bf16[640,2560]{0,1:T(8,128)(2,1)S(1)} %bitcast.45, bf16[640,2560]{1,0:T(8,128)(2,1)S(1)} %bitcast.53), kind=kOutput, calls=%fused_computation.11 | convolution fusion | flops 2097561600 | bytes 7372800 | tf_op jit(solution)/shard_map/dot_general | solution.py:219
  17.9 2.4 %reshape.215 = bf16[32,5,4,640]{3,2,1,0:T(4,128)(2,1)} reshape(bf16[640,640]{1,0:T(8,128)(2,1)} %convolution_convert_fusion) | data formatting | bytes 1638400 | tf_op jit(solution)/shard_map/reshape | solution.py:225
  20.3 7.4 %all-to-all-start = ((bf16[32,5,4,640]{3,2,1,0:T(4,128)(2,1)}), bf16[32,5,4,640]{3,2,1,0:T(4,128)(2,1)}, u32[]{:S(2)}, u32[]{:S(2)}) async-start(bf16[32,5,4,640]{3,2,1,0:T(4,128)(2,1)} %reshape.215), calls=%async_computation | async-start | bytes 1638400 | tf_op jit(solution)/shard_map/all_to_all | solution.py:226
  27.7 0.3 collective-permute-start
  28.0 1.6 collective-permute-start.1
  29.7 1.7 %collective-permute-start.3 = (bf16[80,2560]{1,0:T(8,128)(2,1)}, bf16[80,2560]{1,0:T(8,128)(2,1)}, u32[]{:S(2)}, u32[]{:S(2)}) collective-permute-start(bf16[80,2560]{1,0:T(8,128)(2,1)} %get-tuple-element.42), channel_id=1, source_target_pairs={{0,16},{4,20},{8,24},{12,28},{16,0},{20,4},{24,8},{28,12},{1,17},{... | collective-permute-start | bytes 1228808 | tf_op jit(solution)/shard_map/ppermute | solution.py:206
  31.4 0.1 collective-permute-start.4
  31.5 2.5 %collective-permute-start.5 = (bf16[80,2560]{1,0:T(8,128)(2,1)}, bf16[80,2560]{1,0:T(8,128)(2,1)}, u32[]{:S(2)}, u32[]{:S(2)}) collective-permute-start(bf16[80,2560]{1,0:T(8,128)(2,1)} %get-tuple-element.44), channel_id=1, source_target_pairs={{0,24},{4,28},{8,16},{12,20},{16,8},{20,12},{24,0},{28,4},{1,25},{... | collective-permute-start | bytes 1228808 | tf_op jit(solution)/shard_map/ppermute | solution.py:206
  34.0 14.5 %collective-permute-done.1.refs_3_ = bf16[80,2560]{1,0:T(8,128)(2,1)} collective-permute-done((bf16[80,2560]{1,0:T(8,128)(2,1)}, bf16[80,2560]{1,0:T(8,128)(2,1)}, u32[]{:S(2)}, u32[]{:S(2)}) %collective-permute-start.1) | collective-permute-done | bytes 409632 | tf_op jit(solution)/shard_map/ppermute | solution.py:206
  48.5 5.6 %copy.30.refs_10_.refs_1_ = bf16[640,2560]{1,0:T(8,128)(2,1)} copy(bf16[640,2560]{0,1:T(8,128)(2,1)} %bitcast.44) | data formatting | bytes 6553600 | tf_op jit(solution)/shard_map/optimization_barrier | solution.py:30
  54.1 0.8 constant_dynamic-slice_fusion
  55.0 0.8 copy.41
  55.8 0.6 stack.32.refs_0_
  56.4 0.3 collective-permute-done.4.refs_6_
  56.6 10.5 %collective-permute-done.5.refs_7_ = bf16[80,2560]{1,0:T(8,128)(2,1)} collective-permute-done((bf16[80,2560]{1,0:T(8,128)(2,1)}, bf16[80,2560]{1,0:T(8,128)(2,1)}, u32[]{:S(2)}, u32[]{:S(2)}) %collective-permute-start.5) | collective-permute-done | bytes 409632 | tf_op jit(solution)/shard_map/ppermute | solution.py:206
  67.1 7.6 %collective-permute-done.6.refs_8_ = bf16[80,2560]{1,0:T(8,128)(2,1)} collective-permute-done((bf16[80,2560]{1,0:T(8,128)(2,1)}, bf16[80,2560]{1,0:T(8,128)(2,1)}, u32[]{:S(2)}, u32[]{:S(2)}) %collective-permute-start.6) | collective-permute-done | bytes 409632 | tf_op jit(solution)/shard_map/ppermute | solution.py:206
  74.8 10.5 %score.1 = bf16[160,4,640]{2,1,0:T(4,128)(2,1)} custom-call(s32[8]{0:T(128)} %stack.32.refs_0_, bf16[80,2560]{1,0:T(8,128)(2,1)} %get-tuple-element.38.refs_1_, bf16[80,2560]{1,0:T(8,128)(2,1)} %collective-permute-done.refs_2_, bf16[80,2560]{1,0:T(8,128)(2,1)} %collective-permute-done.1.refs_3_, bf16[80,2560]{1,0:T(8,128)(2,1)} %collective-permute-done.2.refs_4_, ...), custom_call_target="tpu_custom_call" | custom-call | tf_op jit(solution)/shard_map/score/pallas_call | solution.py:125
  85.3 4.3 %all-to-all-start.2 = ((bf16[32,5,4,640]{3,2,1,0:T(4,128)(2,1)}), bf16[32,5,4,640]{3,2,1,0:T(4,128)(2,1)}, u32[]{:S(2)}, u32[]{:S(2)}) async-start(bf16[32,5,4,640]{3,2,1,0:T(4,128)(2,1)} %bitcast.56), calls=%async_computation.2 | async-start | bytes 1638400 | tf_op jit(solution)/shard_map/all_to_all | solution.py:226
  89.6 1.2 copy.31
  90.8 0.9 reshape.217
  91.8 1.7 %copy.32 = bf16[10,8,4,2,4,160]{5,4,3,2,1,0:T(4,128)(2,1)S(1)} copy(bf16[10,8,4,2,4,160]{5,2,1,4,3,0:T(4,128)(2,1)S(1)} %bitcast.48) | data formatting | bytes 1638400 | tf_op jit(solution)/shard_map/transpose | solution.py:246
  93.5 0.8 reshape.218
  94.3 5.6 %fusion.8 = bf16[10,64,640]{2,1,0:T(8,128)(2,1)S(1)} fusion(bf16[80,640,320]{1,2,0:T(8,128)(2,1)} %param.10, s32[]{:T(128)S(6)} %select_n.142, bf16[10,64,640]{2,1,0:T(8,128)(2,1)S(1)} %reshape.218, f32[320]{0:T(512)S(1)} %copy-done.3), kind=kOutput, calls=%fused_computation.9 | convolution fusion | flops 525107200 | bytes 9832704 | tf_op jit(solution)/shard_map/jln,jcn->jcl/dot_general | solution.py:233
  99.9 0.9 reshape.219
  100.8 0.5 copy.33
  101.3 1.9 %reshape.220 = bf16[32,5,4,640]{3,2,1,0:T(4,128)(2,1)} reshape(bf16[4,8,10,2,4,160]{5,4,3,2,1,0:T(4,128)(2,1)S(1)} %copy.33) | data formatting | bytes 1638400 | tf_op jit(solution)/shard_map/reshape | solution.py:238
  103.2 7.4 %all-to-all-done.2 = bf16[32,5,4,640]{3,2,1,0:T(4,128)(2,1)} async-done(((bf16[32,5,4,640]{3,2,1,0:T(4,128)(2,1)}), bf16[32,5,4,640]{3,2,1,0:T(4,128)(2,1)}, u32[]{:S(2)}, u32[]{:S(2)}) %all-to-all-start.2) | async-done | bytes 819232 | tf_op jit(solution)/shard_map/all_to_all | solution.py:226
  110.7 3.7 %all-to-all-start.1 = ((bf16[32,5,4,640]{3,2,1,0:T(4,128)(2,1)}), bf16[32,5,4,640]{3,2,1,0:T(4,128)(2,1)}, u32[]{:S(2)}, u32[]{:S(2)}) async-start(bf16[32,5,4,640]{3,2,1,0:T(4,128)(2,1)} %reshape.220), calls=%async_computation.1 | async-start | bytes 1638400 | tf_op jit(solution)/shard_map/all_to_all | solution.py:226
  114.4 1.2 copy.35
  115.7 1.4 reshape.223
  117.0 1.4 copy.36
  118.5 1.0 reshape.224
  119.5 5.6 %fusion.11 = bf16[10,64,640]{2,1,0:T(8,128)(2,1)S(1)} fusion(bf16[80,640,320]{1,2,0:T(8,128)(2,1)} %param.10, s32[]{:T(128)S(6)} %select_n.142, bf16[10,64,640]{2,1,0:T(8,128)(2,1)S(1)} %reshape.224, f32[320]{0:T(512)S(1)} %copy-done.3), kind=kOutput, calls=%fused_computation.10 | convolution fusion | flops 525107200 | bytes 9832704 | tf_op jit(solution)/shard_map/jln,jcn->jcl/dot_general | solution.py:233
  125.0 0.9 reshape.225
  126.0 0.5 copy.37
  126.5 1.9 %reshape.226 = bf16[32,5,4,640]{3,2,1,0:T(4,128)(2,1)} reshape(bf16[4,8,10,2,4,160]{5,4,3,2,1,0:T(4,128)(2,1)S(1)} %copy.37) | data formatting | bytes 1638400 | tf_op jit(solution)/shard_map/reshape | solution.py:238
  128.4 7.3 %all-to-all-done.1 = bf16[32,5,4,640]{3,2,1,0:T(4,128)(2,1)} async-done(((bf16[32,5,4,640]{3,2,1,0:T(4,128)(2,1)}), bf16[32,5,4,640]{3,2,1,0:T(4,128)(2,1)}, u32[]{:S(2)}, u32[]{:S(2)}) %all-to-all-start.1) | async-done | bytes 819232 | tf_op jit(solution)/shard_map/all_to_all | solution.py:226
  135.7 4.0 %all-to-all-start.3 = ((bf16[32,5,4,640]{3,2,1,0:T(4,128)(2,1)}), bf16[32,5,4,640]{3,2,1,0:T(4,128)(2,1)}, u32[]{:S(2)}, u32[]{:S(2)}) async-start(bf16[32,5,4,640]{3,2,1,0:T(4,128)(2,1)} %reshape.226), calls=%async_computation.3 | async-start | bytes 1638400 | tf_op jit(solution)/shard_map/all_to_all | solution.py:226
  139.6 8.8 %grid.2 = bf16[160,4,2560]{2,1,0:T(4,128)(2,1)} custom-call(bf16[160,4,640]{2,1,0:T(4,128)(2,1)} %bitcast.16.refs_0_, bf16[640,2560]{1,0:T(8,128)(2,1)} %copy.30.refs_10_.refs_1_, bf16[160,4,2560]{2,1,0:T(4,128)(2,1)} %bitcast.54), custom_call_target="tpu_custom_call" | custom-call | tf_op jit(solution)/shard_map/grid/pallas_call | solution.py:174
  148.5 12.3 %all-to-all-done.3 = bf16[32,5,4,640]{3,2,1,0:T(4,128)(2,1)} async-done(((bf16[32,5,4,640]{3,2,1,0:T(4,128)(2,1)}), bf16[32,5,4,640]{3,2,1,0:T(4,128)(2,1)}, u32[]{:S(2)}, u32[]{:S(2)}) %all-to-all-start.3) | async-done | bytes 819232 | tf_op jit(solution)/shard_map/all_to_all | solution.py:226
  160.7 8.1 %grid.3 = bf16[160,4,2560]{2,1,0:T(4,128)(2,1)} custom-call(bf16[160,4,640]{2,1,0:T(4,128)(2,1)} %bitcast.22.refs_0_, bf16[640,2560]{1,0:T(8,128)(2,1)} %copy.30.refs_10_.refs_1_), custom_call_target="tpu_custom_call" | custom-call | tf_op jit(solution)/shard_map/grid/pallas_call | solution.py:174
  (27 shorter events, 0.6 us)
Async XLA Ops:
  0.6 53.5 %copy-start = (bf16[160,4,2560]{2,1,0:T(4,128)(2,1)S(1)}, bf16[160,4,2560]{2,1,0:T(4,128)(2,1)}, u32[]{:S(2)}) copy-start(bf16[160,4,2560]{2,1,0:T(4,128)(2,1)} %param.9) | copy-start | bytes 9830404
  11.3 2.9 %copy-start.2 = (bf16[640,20,128]{0,2,1:T(8,128)(2,1)S(1)}, bf16[640,20,128]{0,2,1:T(8,128)(2,1)}, u32[]{:S(2)}) copy-start(bf16[640,20,128]{0,2,1:T(8,128)(2,1)} %add_convert_fusion) | copy-start | bytes 9830404
  20.3 65.0 %all-to-all-start = ((bf16[32,5,4,640]{3,2,1,0:T(4,128)(2,1)}), bf16[32,5,4,640]{3,2,1,0:T(4,128)(2,1)}, u32[]{:S(2)}, u32[]{:S(2)}) async-start(bf16[32,5,4,640]{3,2,1,0:T(4,128)(2,1)} %reshape.215), calls=%async_computation | async-start | bytes 1638400 | tf_op jit(solution)/shard_map/all_to_all | solution.py:226
  27.7 3.7 %collective-permute-start = (bf16[80,2560]{1,0:T(8,128)(2,1)}, bf16[80,2560]{1,0:T(8,128)(2,1)}, u32[]{:S(2)}, u32[]{:S(2)}) collective-permute-start(bf16[80,2560]{1,0:T(8,128)(2,1)} %get-tuple-element.39), channel_id=1, source_target_pairs={{0,4},{4,0},{8,12},{12,8},{16,20},{20,16},{24,28},{28,24},{1,5},{5... | collective-permute-start | bytes 1228808 | tf_op jit(solution)/shard_map/ppermute | solution.py:206
  28.0 20.5 %collective-permute-start.1 = (bf16[80,2560]{1,0:T(8,128)(2,1)}, bf16[80,2560]{1,0:T(8,128)(2,1)}, u32[]{:S(2)}, u32[]{:S(2)}) collective-permute-start(bf16[80,2560]{1,0:T(8,128)(2,1)} %get-tuple-element.40), channel_id=1, source_target_pairs={{0,8},{4,12},{8,0},{12,4},{16,24},{20,28},{24,16},{28,20},{1,9},{5... | collective-permute-start | bytes 1228808 | tf_op jit(solution)/shard_map/ppermute | solution.py:206
  29.6 26.7 %collective-permute-start.2 = (bf16[80,2560]{1,0:T(8,128)(2,1)}, bf16[80,2560]{1,0:T(8,128)(2,1)}, u32[]{:S(2)}, u32[]{:S(2)}) collective-permute-start(bf16[80,2560]{1,0:T(8,128)(2,1)} %get-tuple-element.41), channel_id=1, source_target_pairs={{0,12},{4,8},{8,4},{12,0},{16,28},{20,24},{24,20},{28,16},{1,13},{... | collective-permute-start | bytes 1228808 | tf_op jit(solution)/shard_map/ppermute | solution.py:206
  29.7 26.7 %collective-permute-start.3 = (bf16[80,2560]{1,0:T(8,128)(2,1)}, bf16[80,2560]{1,0:T(8,128)(2,1)}, u32[]{:S(2)}, u32[]{:S(2)}) collective-permute-start(bf16[80,2560]{1,0:T(8,128)(2,1)} %get-tuple-element.42), channel_id=1, source_target_pairs={{0,16},{4,20},{8,24},{12,28},{16,0},{20,4},{24,8},{28,12},{1,17},{... | collective-permute-start | bytes 1228808 | tf_op jit(solution)/shard_map/ppermute | solution.py:206
  31.4 25.3 %collective-permute-start.4 = (bf16[80,2560]{1,0:T(8,128)(2,1)}, bf16[80,2560]{1,0:T(8,128)(2,1)}, u32[]{:S(2)}, u32[]{:S(2)}) collective-permute-start(bf16[80,2560]{1,0:T(8,128)(2,1)} %get-tuple-element.43), channel_id=1, source_target_pairs={{0,20},{4,16},{8,28},{12,24},{16,4},{20,0},{24,12},{28,8},{1,21},{... | collective-permute-start | bytes 1228808 | tf_op jit(solution)/shard_map/ppermute | solution.py:206
  31.5 35.7 %collective-permute-start.5 = (bf16[80,2560]{1,0:T(8,128)(2,1)}, bf16[80,2560]{1,0:T(8,128)(2,1)}, u32[]{:S(2)}, u32[]{:S(2)}) collective-permute-start(bf16[80,2560]{1,0:T(8,128)(2,1)} %get-tuple-element.44), channel_id=1, source_target_pairs={{0,24},{4,28},{8,16},{12,20},{16,8},{20,12},{24,0},{28,4},{1,25},{... | collective-permute-start | bytes 1228808 | tf_op jit(solution)/shard_map/ppermute | solution.py:206
  48.5 26.2 %collective-permute-start.6 = (bf16[80,2560]{1,0:T(8,128)(2,1)}, bf16[80,2560]{1,0:T(8,128)(2,1)}, u32[]{:S(2)}, u32[]{:S(2)}) collective-permute-start(bf16[80,2560]{1,0:T(8,128)(2,1)} %get-tuple-element.45), channel_id=1, source_target_pairs={{0,28},{4,24},{8,20},{12,16},{16,12},{20,8},{24,4},{28,0},{1,29},{... | collective-permute-start | bytes 1228808 | tf_op jit(solution)/shard_map/ppermute | solution.py:206
  85.3 25.4 %all-to-all-start.2 = ((bf16[32,5,4,640]{3,2,1,0:T(4,128)(2,1)}), bf16[32,5,4,640]{3,2,1,0:T(4,128)(2,1)}, u32[]{:S(2)}, u32[]{:S(2)}) async-start(bf16[32,5,4,640]{3,2,1,0:T(4,128)(2,1)} %bitcast.56), calls=%async_computation.2 | async-start | bytes 1638400 | tf_op jit(solution)/shard_map/all_to_all | solution.py:226
  90.8 3.5 %copy-start.3 = (f32[320]{0:T(512)S(1)}, f32[320]{0:T(512)}, u32[]{:S(2)}) copy-start(f32[320]{0:T(512)} %param.11) | copy-start | bytes 3844
  110.7 25.0 %all-to-all-start.1 = ((bf16[32,5,4,640]{3,2,1,0:T(4,128)(2,1)}), bf16[32,5,4,640]{3,2,1,0:T(4,128)(2,1)}, u32[]{:S(2)}, u32[]{:S(2)}) async-start(bf16[32,5,4,640]{3,2,1,0:T(4,128)(2,1)} %reshape.220), calls=%async_computation.1 | async-start | bytes 1638400 | tf_op jit(solution)/shard_map/all_to_all | solution.py:226
  135.7 25.0 %all-to-all-start.3 = ((bf16[32,5,4,640]{3,2,1,0:T(4,128)(2,1)}), bf16[32,5,4,640]{3,2,1,0:T(4,128)(2,1)}, u32[]{:S(2)}, u32[]{:S(2)}) async-start(bf16[32,5,4,640]{3,2,1,0:T(4,128)(2,1)} %reshape.226), calls=%async_computation.3 | async-start | bytes 1638400 | tf_op jit(solution)/shard_map/all_to_all | solution.py:226
  160.7 8.1 %copy-start.1 = (bf16[160,4,2560]{2,1,0:T(4,128)(2,1)S(1)}, bf16[160,4,2560]{2,1,0:T(4,128)(2,1)}, u32[]{:S(2)}) copy-start(bf16[160,4,2560]{2,1,0:T(4,128)(2,1)} %param.9) | copy-start | bytes 9830404

commit v3 on v2

--- a/solution.py
+++ b/solution.py
@@ -169,7 +169,7 @@
 
 def to_grid(coeffs, table, added, rows, levels):
     cols, lon = table.shape
-    step = 512 if lon % 512 == 0 else lon
+    step = 1280 if lon % 1280 == 0 else lon
     block = pl.BlockSpec((rows, levels, step), lambda i: (0, 0, i))
     return pl.pallas_call(
         lambda *refs: grid_kernel(rows, levels, *refs),
@@ -182,6 +182,7 @@
         + [block] * (added is not None),
         out_specs=block,
         scratch_shapes=[pltpu.VMEM((rows * levels, cols), jnp.bfloat16)],
+        compiler_params=pltpu.CompilerParams(vmem_limit_bytes=56 * 2**20),
         name="grid",
     )(coeffs.reshape(cols // 4, 4, rows * levels), table, *([added] if added is not None else []))
 
@@ -201,7 +202,7 @@
         sent = split(outlook[0], me, members)
         sent, start = lax.optimization_barrier((sent, start))
         blocks, slots = [sent[0]], [me]
-        for s in range(1, members):
+        for s in range(members - 1, 0, -1):
             blocks.append(
                 lax.ppermute(sent[s], "member", [(a, a ^ s) for a in range(members)])
             )

time: 170 us -> 170 us (level)
  Pallas kernels: 33 us -> 30.5 us
    pallas_call x2, Pallas kernels: 16.9 us -> 14.3 us  [to_grid(): pl.pallas_call(lambda *refs: grid_kernel(rows, levels, *refs), out_shape=...]
where the time goes in v3:
time: 170 us; the launch traced here: 169 us
  waiting for transfers between devices  61.5 us (36%)
  Pallas kernels  30.5 us (18%)
  local copies, waits for them, and re-layouts  30.1 us (18%)
  starting transfers between devices  26.8 us (16%)
  matrix products  14.8 us (9%)
  other arithmetic  4.35 us (3%)
    ppermute x7, waiting for transfers between devices, work(): lax.ppermute(sent[s], 'member', [(a, a ^ s) for a in range(members)])  33 us
    all_to_all x4, waiting for transfers between devices, to_waves(): return lax.all_to_all(coeffs, both, 0, 0, tiled=True)  28.4 us
    all_to_all x4, starting transfers between devices, to_waves(): return lax.all_to_all(coeffs, both, 0, 0, tiled=True)  20.2 us
    pallas_call x2, Pallas kernels, to_grid(): pl.pallas_call(lambda *refs: grid_kernel(rows, levels, *refs), out_shape=...  14.3 us
    dot_general x2, matrix products, legendre(): jnp.einsum('jln,jcn->jcl', mine, spectra, preferred_element_type=jnp.floa...  11.1 us
    pallas_call x1, Pallas kernels, score_coeffs(): pl.pallas_call(lambda *refs: score_kernel(members, *refs), out_shape=jax....  10.5 us
    ppermute x7, starting transfers between devices, work(): lax.ppermute(sent[s], 'member', [(a, a ^ s) for a in range(members)])  6.59 us
    pallas_call x1, Pallas kernels, split(): pl.pallas_call(lambda *refs: split_kernel(halves, *refs), out_shape=[jax....  5.67 us
  transfers between devices with their start and end apart: 11, of which 7 were waited for; matrix products, arithmetic and copies ran while one was open for 21% of the time, Pallas kernels for 11%

profile of v3, /device:TPU:0, one launch (start us, length us, event | category | flops | bytes accessed | tf_op | source)
XLA Modules:
  0.0 168.9 jit_solution(6888643133319315716)
XLA Ops:
  1.3 1.3 fusion.36
  2.7 0.3 select_multiply_fusion
  3.0 2.6 %add_convert_fusion = bf16[640,20,128]{0,2,1:T(8,128)(2,1)} fusion(f32[640,128]{0,1:T(8,128)S(1)} %get-tuple-element.28, f32[640,20]{0,1:T(8,128)S(1)} %get-tuple-element.27, f32[640,128]{0,1:T(8,128)S(1)} %get-tuple-element.26, f32[640,20]{0,1:T(8,128)S(1)} %get-tuple-element.25), kind=kLoop, calls=%fused_computation | loop fusion | flops 6553600 | bytes 4034560 | tf_op jit(solution)/shard_map/convert_element_type | solution.py:30
  5.6 5.7 %split.1 = (bf16[80,2560]{1,0:T(8,128)(2,1)}, bf16[80,2560]{1,0:T(8,128)(2,1)}, bf16[80,2560]{1,0:T(8,128)(2,1)}, bf16[80,2560]{1,0:T(8,128)(2,1)}, bf16[80,2560...) custom-call(s32[1]{0:T(128)} %bitcast.1.refs_0_, ...), custom_call_target="tpu_custom_call" | custom-call | tf_op jit(solution)/shard_map/split/pallas_call | solution.py:56
  11.3 2.6 %copy.28 = bf16[1,160,4,2560]{3,1,2,0:T(8,128)(2,1)S(1)} copy(bf16[1,160,4,2560]{3,2,1,0:T(4,128)(2,1)} %param.6) | data formatting | bytes 6553600 | tf_op jit(solution)/shard_map/optimization_barrier | solution.py:203
  14.0 0.3 copy-done.2
  14.2 3.6 %convolution_convert_fusion = bf16[640,640]{1,0:T(8,128)(2,1)} fusion(bf16[640,2560]{0,1:T(8,128)(2,1)S(1)} %bitcast.45, bf16[640,2560]{1,0:T(8,128)(2,1)S(1)} %bitcast.53), kind=kOutput, calls=%fused_computation.11 | convolution fusion | flops 2097561600 | bytes 7372800 | tf_op jit(solution)/shard_map/dot_general | solution.py:220
  17.9 2.4 %reshape.215 = bf16[32,5,4,640]{3,2,1,0:T(4,128)(2,1)} reshape(bf16[640,640]{1,0:T(8,128)(2,1)} %convolution_convert_fusion) | data formatting | bytes 1638400 | tf_op jit(solution)/shard_map/reshape | solution.py:226
  20.3 7.4 %all-to-all-start = ((bf16[32,5,4,640]{3,2,1,0:T(4,128)(2,1)}), bf16[32,5,4,640]{3,2,1,0:T(4,128)(2,1)}, u32[]{:S(2)}, u32[]{:S(2)}) async-start(bf16[32,5,4,640]{3,2,1,0:T(4,128)(2,1)} %reshape.215), calls=%async_computation | async-start | bytes 1638400 | tf_op jit(solution)/shard_map/all_to_all | solution.py:227
  27.7 2.4 %collective-permute-start = (bf16[80,2560]{1,0:T(8,128)(2,1)}, bf16[80,2560]{1,0:T(8,128)(2,1)}, u32[]{:S(2)}, u32[]{:S(2)}) collective-permute-start(bf16[80,2560]{1,0:T(8,128)(2,1)} %get-tuple-element.39), channel_id=1, source_target_pairs={{0,28},{4,24},{8,20},{12,16},{16,12},{20,8},{24,4},{28,0},{1,29},{... | collective-permute-start | bytes 1228808 | tf_op jit(solution)/shard_map/ppermute | solution.py:207
  30.1 0.4 collective-permute-start.1
  30.5 1.4 collective-permute-start.2
  31.9 0.3 collective-permute-start.3
  32.2 1.4 collective-permute-start.4
  33.6 15.6 %collective-permute-done.refs_2_ = bf16[80,2560]{1,0:T(8,128)(2,1)} collective-permute-done((bf16[80,2560]{1,0:T(8,128)(2,1)}, bf16[80,2560]{1,0:T(8,128)(2,1)}, u32[]{:S(2)}, u32[]{:S(2)}) %collective-permute-start) | collective-permute-done | bytes 409632 | tf_op jit(solution)/shard_map/ppermute | solution.py:207
  49.2 0.7 collective-permute-start.5
  49.9 9.2 %collective-permute-done.1.refs_3_ = bf16[80,2560]{1,0:T(8,128)(2,1)} collective-permute-done((bf16[80,2560]{1,0:T(8,128)(2,1)}, bf16[80,2560]{1,0:T(8,128)(2,1)}, u32[]{:S(2)}, u32[]{:S(2)}) %collective-permute-start.1) | collective-permute-done | bytes 409632 | tf_op jit(solution)/shard_map/ppermute | solution.py:207
  59.1 5.6 %copy.30.refs_10_.refs_1_ = bf16[640,2560]{1,0:T(8,128)(2,1)} copy(bf16[640,2560]{0,1:T(8,128)(2,1)} %bitcast.44) | data formatting | bytes 6553600 | tf_op jit(solution)/shard_map/optimization_barrier | solution.py:30
  64.7 0.8 constant_dynamic-slice_fusion
  65.6 0.8 copy.41
  66.4 0.6 stack.32.refs_0_
  67.0 7.8 %collective-permute-done.3.refs_5_ = bf16[80,2560]{1,0:T(8,128)(2,1)} collective-permute-done((bf16[80,2560]{1,0:T(8,128)(2,1)}, bf16[80,2560]{1,0:T(8,128)(2,1)}, u32[]{:S(2)}, u32[]{:S(2)}) %collective-permute-start.3) | collective-permute-done | bytes 409632 | tf_op jit(solution)/shard_map/ppermute | solution.py:207
  74.8 0.4 collective-permute-done.5.refs_7_
  75.2 10.5 %score.1 = bf16[160,4,640]{2,1,0:T(4,128)(2,1)} custom-call(s32[8]{0:T(128)} %stack.32.refs_0_, bf16[80,2560]{1,0:T(8,128)(2,1)} %get-tuple-element.38.refs_1_, bf16[80,2560]{1,0:T(8,128)(2,1)} %collective-permute-done.refs_2_, bf16[80,2560]{1,0:T(8,128)(2,1)} %collective-permute-done.1.refs_3_, bf16[80,2560]{1,0:T(8,128)(2,1)} %collective-permute-done.2.refs_4_, ...), custom_call_target="tpu_custom_call" | custom-call | tf_op jit(solution)/shard_map/score/pallas_call | solution.py:125
  85.8 5.1 %all-to-all-start.2 = ((bf16[32,5,4,640]{3,2,1,0:T(4,128)(2,1)}), bf16[32,5,4,640]{3,2,1,0:T(4,128)(2,1)}, u32[]{:S(2)}, u32[]{:S(2)}) async-start(bf16[32,5,4,640]{3,2,1,0:T(4,128)(2,1)} %bitcast.56), calls=%async_computation.2 | async-start | bytes 1638400 | tf_op jit(solution)/shard_map/all_to_all | solution.py:227
  90.8 1.2 copy.31
  92.1 0.9 reshape.217
  93.0 1.7 %copy.32 = bf16[10,8,4,2,4,160]{5,4,3,2,1,0:T(4,128)(2,1)S(1)} copy(bf16[10,8,4,2,4,160]{5,2,1,4,3,0:T(4,128)(2,1)S(1)} %bitcast.48) | data formatting | bytes 1638400 | tf_op jit(solution)/shard_map/transpose | solution.py:247
  94.7 0.8 reshape.218
  95.6 5.6 %fusion.8 = bf16[10,64,640]{2,1,0:T(8,128)(2,1)S(1)} fusion(bf16[80,640,320]{1,2,0:T(8,128)(2,1)} %param.10, s32[]{:T(128)S(6)} %select_n.142, bf16[10,64,640]{2,1,0:T(8,128)(2,1)S(1)} %reshape.218, f32[320]{0:T(512)S(1)} %copy-done.3), kind=kOutput, calls=%fused_computation.9 | convolution fusion | flops 525107200 | bytes 9832704 | tf_op jit(solution)/shard_map/jln,jcn->jcl/dot_general | solution.py:234
  101.2 0.9 reshape.219
  102.1 0.5 copy.33
  102.6 1.9 %reshape.220 = bf16[32,5,4,640]{3,2,1,0:T(4,128)(2,1)} reshape(bf16[4,8,10,2,4,160]{5,4,3,2,1,0:T(4,128)(2,1)S(1)} %copy.33) | data formatting | bytes 1638400 | tf_op jit(solution)/shard_map/reshape | solution.py:239
  104.5 7.4 %all-to-all-done.2 = bf16[32,5,4,640]{3,2,1,0:T(4,128)(2,1)} async-done(((bf16[32,5,4,640]{3,2,1,0:T(4,128)(2,1)}), bf16[32,5,4,640]{3,2,1,0:T(4,128)(2,1)}, u32[]{:S(2)}, u32[]{:S(2)}) %all-to-all-start.2) | async-done | bytes 819232 | tf_op jit(solution)/shard_map/all_to_all | solution.py:227
  111.9 3.7 %all-to-all-start.1 = ((bf16[32,5,4,640]{3,2,1,0:T(4,128)(2,1)}), bf16[32,5,4,640]{3,2,1,0:T(4,128)(2,1)}, u32[]{:S(2)}, u32[]{:S(2)}) async-start(bf16[32,5,4,640]{3,2,1,0:T(4,128)(2,1)} %reshape.220), calls=%async_computation.1 | async-start | bytes 1638400 | tf_op jit(solution)/shard_map/all_to_all | solution.py:227
  115.7 1.2 copy.35
  116.9 1.4 reshape.223
  118.3 1.4 copy.36
  119.7 1.0 reshape.224
  120.7 5.6 %fusion.11 = bf16[10,64,640]{2,1,0:T(8,128)(2,1)S(1)} fusion(bf16[80,640,320]{1,2,0:T(8,128)(2,1)} %param.10, s32[]{:T(128)S(6)} %select_n.142, bf16[10,64,640]{2,1,0:T(8,128)(2,1)S(1)} %reshape.224, f32[320]{0:T(512)S(1)} %copy-done.3), kind=kOutput, calls=%fused_computation.10 | convolution fusion | flops 525107200 | bytes 9832704 | tf_op jit(solution)/shard_map/jln,jcn->jcl/dot_general | solution.py:234
  126.3 0.9 reshape.225
  127.2 0.5 copy.37
  127.8 1.9 %reshape.226 = bf16[32,5,4,640]{3,2,1,0:T(4,128)(2,1)} reshape(bf16[4,8,10,2,4,160]{5,4,3,2,1,0:T(4,128)(2,1)S(1)} %copy.37) | data formatting | bytes 1638400 | tf_op jit(solution)/shard_map/reshape | solution.py:239
  129.7 7.3 %all-to-all-done.1 = bf16[32,5,4,640]{3,2,1,0:T(4,128)(2,1)} async-done(((bf16[32,5,4,640]{3,2,1,0:T(4,128)(2,1)}), bf16[32,5,4,640]{3,2,1,0:T(4,128)(2,1)}, u32[]{:S(2)}, u32[]{:S(2)}) %all-to-all-start.1) | async-done | bytes 819232 | tf_op jit(solution)/shard_map/all_to_all | solution.py:227
  137.0 4.0 %all-to-all-start.3 = ((bf16[32,5,4,640]{3,2,1,0:T(4,128)(2,1)}), bf16[32,5,4,640]{3,2,1,0:T(4,128)(2,1)}, u32[]{:S(2)}, u32[]{:S(2)}) async-start(bf16[32,5,4,640]{3,2,1,0:T(4,128)(2,1)} %reshape.226), calls=%async_computation.3 | async-start | bytes 1638400 | tf_op jit(solution)/shard_map/all_to_all | solution.py:227
  140.9 7.4 %grid.2 = bf16[160,4,2560]{2,1,0:T(4,128)(2,1)} custom-call(bf16[160,4,640]{2,1,0:T(4,128)(2,1)} %bitcast.16.refs_0_, bf16[640,2560]{1,0:T(8,128)(2,1)} %copy.30.refs_10_.refs_1_, bf16[160,4,2560]{2,1,0:T(4,128)(2,1)} %bitcast.54), custom_call_target="tpu_custom_call" | custom-call | tf_op jit(solution)/shard_map/grid/pallas_call | solution.py:174
  148.3 13.6 %all-to-all-done.3 = bf16[32,5,4,640]{3,2,1,0:T(4,128)(2,1)} async-done(((bf16[32,5,4,640]{3,2,1,0:T(4,128)(2,1)}), bf16[32,5,4,640]{3,2,1,0:T(4,128)(2,1)}, u32[]{:S(2)}, u32[]{:S(2)}) %all-to-all-start.3) | async-done | bytes 819232 | tf_op jit(solution)/shard_map/all_to_all | solution.py:227
  162.0 6.9 %grid.3 = bf16[160,4,2560]{2,1,0:T(4,128)(2,1)} custom-call(bf16[160,4,640]{2,1,0:T(4,128)(2,1)} %bitcast.22.refs_0_, bf16[640,2560]{1,0:T(8,128)(2,1)} %copy.30.refs_10_.refs_1_), custom_call_target="tpu_custom_call" | custom-call | tf_op jit(solution)/shard_map/grid/pallas_call | solution.py:174
  (27 shorter events, 0.6 us)
Async XLA Ops:
  0.6 64.1 %copy-start = (bf16[160,4,2560]{2,1,0:T(4,128)(2,1)S(1)}, bf16[160,4,2560]{2,1,0:T(4,128)(2,1)}, u32[]{:S(2)}) copy-start(bf16[160,4,2560]{2,1,0:T(4,128)(2,1)} %param.9) | copy-start | bytes 9830404
  11.3 2.9 %copy-start.2 = (bf16[640,20,128]{0,2,1:T(8,128)(2,1)S(1)}, bf16[640,20,128]{0,2,1:T(8,128)(2,1)}, u32[]{:S(2)}) copy-start(bf16[640,20,128]{0,2,1:T(8,128)(2,1)} %add_convert_fusion) | copy-start | bytes 9830404
  20.3 65.5 %all-to-all-start = ((bf16[32,5,4,640]{3,2,1,0:T(4,128)(2,1)}), bf16[32,5,4,640]{3,2,1,0:T(4,128)(2,1)}, u32[]{:S(2)}, u32[]{:S(2)}) async-start(bf16[32,5,4,640]{3,2,1,0:T(4,128)(2,1)} %reshape.215), calls=%async_computation | async-start | bytes 1638400 | tf_op jit(solution)/shard_map/all_to_all | solution.py:227
  27.7 21.4 %collective-permute-start = (bf16[80,2560]{1,0:T(8,128)(2,1)}, bf16[80,2560]{1,0:T(8,128)(2,1)}, u32[]{:S(2)}, u32[]{:S(2)}) collective-permute-start(bf16[80,2560]{1,0:T(8,128)(2,1)} %get-tuple-element.39), channel_id=1, source_target_pairs={{0,28},{4,24},{8,20},{12,16},{16,12},{20,8},{24,4},{28,0},{1,29},{... | collective-permute-start | bytes 1228808 | tf_op jit(solution)/shard_map/ppermute | solution.py:207
  30.1 29.0 %collective-permute-start.1 = (bf16[80,2560]{1,0:T(8,128)(2,1)}, bf16[80,2560]{1,0:T(8,128)(2,1)}, u32[]{:S(2)}, u32[]{:S(2)}) collective-permute-start(bf16[80,2560]{1,0:T(8,128)(2,1)} %get-tuple-element.40), channel_id=1, source_target_pairs={{0,24},{4,28},{8,16},{12,20},{16,8},{20,12},{24,0},{28,4},{1,25},{... | collective-permute-start | bytes 1228808 | tf_op jit(solution)/shard_map/ppermute | solution.py:207
  30.5 36.4 %collective-permute-start.2 = (bf16[80,2560]{1,0:T(8,128)(2,1)}, bf16[80,2560]{1,0:T(8,128)(2,1)}, u32[]{:S(2)}, u32[]{:S(2)}) collective-permute-start(bf16[80,2560]{1,0:T(8,128)(2,1)} %get-tuple-element.41), channel_id=1, source_target_pairs={{0,20},{4,16},{8,28},{12,24},{16,4},{20,0},{24,12},{28,8},{1,21},{... | collective-permute-start | bytes 1228808 | tf_op jit(solution)/shard_map/ppermute | solution.py:207
  31.9 42.9 %collective-permute-start.3 = (bf16[80,2560]{1,0:T(8,128)(2,1)}, bf16[80,2560]{1,0:T(8,128)(2,1)}, u32[]{:S(2)}, u32[]{:S(2)}) collective-permute-start(bf16[80,2560]{1,0:T(8,128)(2,1)} %get-tuple-element.42), channel_id=1, source_target_pairs={{0,16},{4,20},{8,24},{12,28},{16,0},{20,4},{24,8},{28,12},{1,17},{... | collective-permute-start | bytes 1228808 | tf_op jit(solution)/shard_map/ppermute | solution.py:207
  32.2 42.6 %collective-permute-start.4 = (bf16[80,2560]{1,0:T(8,128)(2,1)}, bf16[80,2560]{1,0:T(8,128)(2,1)}, u32[]{:S(2)}, u32[]{:S(2)}) collective-permute-start(bf16[80,2560]{1,0:T(8,128)(2,1)} %get-tuple-element.43), channel_id=1, source_target_pairs={{0,12},{4,8},{8,4},{12,0},{16,28},{20,24},{24,20},{28,16},{1,13},{... | collective-permute-start | bytes 1228808 | tf_op jit(solution)/shard_map/ppermute | solution.py:207
  49.2 26.0 %collective-permute-start.5 = (bf16[80,2560]{1,0:T(8,128)(2,1)}, bf16[80,2560]{1,0:T(8,128)(2,1)}, u32[]{:S(2)}, u32[]{:S(2)}) collective-permute-start(bf16[80,2560]{1,0:T(8,128)(2,1)} %get-tuple-element.44), channel_id=1, source_target_pairs={{0,8},{4,12},{8,0},{12,4},{16,24},{20,28},{24,16},{28,20},{1,9},{5... | collective-permute-start | bytes 1228808 | tf_op jit(solution)/shard_map/ppermute | solution.py:207
  59.1 16.1 %collective-permute-start.6 = (bf16[80,2560]{1,0:T(8,128)(2,1)}, bf16[80,2560]{1,0:T(8,128)(2,1)}, u32[]{:S(2)}, u32[]{:S(2)}) collective-permute-start(bf16[80,2560]{1,0:T(8,128)(2,1)} %get-tuple-element.45), channel_id=1, source_target_pairs={{0,4},{4,0},{8,12},{12,8},{16,20},{20,16},{24,28},{28,24},{1,5},{5... | collective-permute-start | bytes 1228808 | tf_op jit(solution)/shard_map/ppermute | solution.py:207
  85.8 26.2 %all-to-all-start.2 = ((bf16[32,5,4,640]{3,2,1,0:T(4,128)(2,1)}), bf16[32,5,4,640]{3,2,1,0:T(4,128)(2,1)}, u32[]{:S(2)}, u32[]{:S(2)}) async-start(bf16[32,5,4,640]{3,2,1,0:T(4,128)(2,1)} %bitcast.56), calls=%async_computation.2 | async-start | bytes 1638400 | tf_op jit(solution)/shard_map/all_to_all | solution.py:227
  92.1 3.5 %copy-start.3 = (f32[320]{0:T(512)S(1)}, f32[320]{0:T(512)}, u32[]{:S(2)}) copy-start(f32[320]{0:T(512)} %param.11) | copy-start | bytes 3844
  111.9 25.0 %all-to-all-start.1 = ((bf16[32,5,4,640]{3,2,1,0:T(4,128)(2,1)}), bf16[32,5,4,640]{3,2,1,0:T(4,128)(2,1)}, u32[]{:S(2)}, u32[]{:S(2)}) async-start(bf16[32,5,4,640]{3,2,1,0:T(4,128)(2,1)} %reshape.220), calls=%async_computation.1 | async-start | bytes 1638400 | tf_op jit(solution)/shard_map/all_to_all | solution.py:227
  137.0 25.0 %all-to-all-start.3 = ((bf16[32,5,4,640]{3,2,1,0:T(4,128)(2,1)}), bf16[32,5,4,640]{3,2,1,0:T(4,128)(2,1)}, u32[]{:S(2)}, u32[]{:S(2)}) async-start(bf16[32,5,4,640]{3,2,1,0:T(4,128)(2,1)} %reshape.226), calls=%async_computation.3 | async-start | bytes 1638400 | tf_op jit(solution)/shard_map/all_to_all | solution.py:227
  162.0 6.9 %copy-start.1 = (bf16[160,4,2560]{2,1,0:T(4,128)(2,1)S(1)}, bf16[160,4,2560]{2,1,0:T(4,128)(2,1)}, u32[]{:S(2)}) copy-start(bf16[160,4,2560]{2,1,0:T(4,128)(2,1)} %param.9) | copy-start | bytes 9830404
